TPU v7x, 128 devices: a whole 4x4x4 slice. The times are simulated.
128 devices in a mesh: dev: 8 (over z_hi, y), ma: 16 (over z_lo, x, core).
Axes of the slice: x: 4, y: 4, z: 4 (z_hi: 2, z_lo: 2; z = z_hi * 2 + z_lo), core: 2. Of those that a mesh axis runs over, the one named last changes fastest.
Arguments:
- joined_weight: bfloat16 [8, 4096, 6144], P(None, 'dev', 'ma'), may hold values from -6 to 6
- norm_gain: float32 [8, 4096], P(None, 'ma'), may hold values from 0.5 to 1.5
- rotary_order: int32 [128], replicated, may hold values from 0 to 127, each once
Outputs:
- query_weight: bfloat16 [8, 4096, 4096], P(None, 'dev', 'ma')
- key_weight: bfloat16 [8, 1024, 4096], P(None, 'dev', 'ma')
- value_weight: bfloat16 [8, 1024, 4096], P(None, 'dev', 'ma')
- row_peak: float32 [8, 6144], P(None, 'dev')
Inputs may be any that keep to these rules, and one draw needn't show every extreme that they name: rotary_order holds every number of 0 to 127 exactly once.
All inputs are finite; a program needn't handle non-finite values.
Results may differ from a plain program's by a relative error of at most 0.0055.
Values may be sent and summed in bfloat16 or wider, within the bound.
A program may use at most 128 MiB of HBM per device.

v0:
```python
import jax
import jax.numpy as jnp
from jax import lax
from jax.sharding import PartitionSpec as P

HEADS = 32
KV_HEADS = 8
GROUP = 4


def over_pieces(array, axis):
    return lax.all_gather(array, axis).max(0)


def arrange(stored):
    layer_count, row_count, column_count = stored.shape
    head_total = HEADS + 2 * KV_HEADS
    split = stored.reshape(layer_count, row_count, column_count // head_total, head_total)
    slots_query = split[..., :HEADS].reshape(layer_count, row_count, -1, KV_HEADS, GROUP)
    slots_key = split[..., HEADS : HEADS + KV_HEADS][..., None]
    slots_value = split[..., HEADS + KV_HEADS :][..., None]
    grouped = jnp.concatenate([slots_query, slots_key, slots_value], axis=4)
    return grouped


def settle(moved):
    return jnp.transpose(moved, (0, 3, 4, 2, 1))


def finish_tiles(canonical, gain_rows, rotary_order):
    layer_count = canonical.shape[0]
    column_count = canonical.shape[4]
    turned = jnp.take(canonical[:, :, : GROUP + 1], rotary_order, axis=3)
    complete = jnp.concatenate([turned, canonical[:, :, GROUP + 1 :]], axis=2)
    scaled = (complete.astype(jnp.float32) * gain_rows[:, None, None, None, :]).astype(jnp.bfloat16)
    query_rows = scaled[:, :, :GROUP].reshape(layer_count, -1, column_count)
    key_rows = scaled[:, :, GROUP].reshape(layer_count, -1, column_count)
    value_rows = scaled[:, :, GROUP + 1].reshape(layer_count, -1, column_count)
    local_peak = jnp.max(jnp.abs(scaled.astype(jnp.float32)), axis=4).reshape(layer_count, -1)
    return (query_rows, key_rows, value_rows, local_peak)


def shards(joined_weight, norm_gain, rotary_order):
    first_split, first_concat = (3, 1)
    second_split, second_concat = (1, 2)
    prepared = arrange(joined_weight)
    grouped = lax.all_to_all(
        prepared, "dev", split_axis=first_split, concat_axis=first_concat, tiled=True
    )
    moved = lax.all_to_all(
        grouped, "ma", split_axis=second_split, concat_axis=second_concat, tiled=True
    )
    query_rows, key_rows, value_rows, local_peak = finish_tiles(
        settle(moved), norm_gain, rotary_order
    )
    row_peak = over_pieces(local_peak, "ma")
    return (query_rows, key_rows, value_rows, row_peak)


def solution(mesh):
    placed = (P(None, "dev", "ma"), P(None, "ma"), P())
    return jax.shard_map(
        shards,
        mesh=mesh,
        in_specs=placed,
        out_specs=(
            P(None, "dev", "ma"),
            P(None, "dev", "ma"),
            P(None, "dev", "ma"),
            P(None, "dev"),
        ),
        check_vma=False,
    )
```

profile of v0, /device:TPU:1, one launch (start us, length us, event | category | flops | bytes accessed | tf_op | source)
XLA Modules:
  0.0 354.9 jit_solution(11645745787527981366)
XLA Ops:
  0.6 3.2 copy.33
  3.8 0.1 slice_bitcast_fusion.4
  3.9 0.2 slice.34
  4.2 0.2 copy.35
  4.3 0.2 copy.36
  4.5 1.2 copy.34
  5.8 0.4 pad_maximum_fusion
  6.1 0.3 copy.37
  6.4 61.3 %all_to_all.36 = bf16[8,512,8,8,6]{1,2,4,0,3:T(8,128)(2,1)S(1)} all-to-all(bf16[8,512,8,8,6]{1,2,4,0,3:T(8,128)(2,1)S(1)} %copy.37), channel_id=1, replica_groups=mesh['dev'=8,'ma'=16] {'dev'}, dimensions={3} | all-to-all | bytes 6291456 | tf_op jit(solution)/shard_map/all_to_all | solution.py:47
  67.8 47.9 %copy.47 = bf16[8,8,512,8,1,6]{3,0,5,2,1,4:T(8,128)(2,1)} copy(bf16[8,8,512,8,1,6]{2,3,5,0,1,4:T(8,128)(2,1)S(1)} %bitcast.31) | data formatting | bytes 6291456 | tf_op jit(solution)/shard_map/all_to_all | solution.py:47
  115.7 57.5 %reshape.100 = bf16[16,2,49152]{2,1,0:T(2,128)(2,1)} reshape(bf16[4096,1,6,8,8]{4,3,2,1,0:T(8,128)(2,1)} %bitcast.29) | data formatting | bytes 6291456
  173.1 0.0 copy-start.1
  173.1 6.0 %all-to-all-start.1 = ((bf16[16,2,49152]{2,1,0:T(2,128)(2,1)}), bf16[16,2,49152]{2,1,0:T(2,128)(2,1)S(1)}, u32[]{:S(2)}, u32[]{:S(2)}) async-start(bf16[16,2,49152]{2,1,0:T(2,128)(2,1)} %reshape.100), calls=%async_computation.1 | async-start | bytes 6291456 | tf_op jit(solution)/shard_map/all_to_all | solution.py:50
  179.1 0.0 copy-done.1
  179.2 42.1 %all-to-all-done.1 = bf16[16,2,49152]{2,1,0:T(2,128)(2,1)S(1)} async-done(((bf16[16,2,49152]{2,1,0:T(2,128)(2,1)}), bf16[16,2,49152]{2,1,0:T(2,128)(2,1)S(1)}, u32[]{:S(2)}, u32[]{:S(2)}) %all-to-all-start.1) | async-done | bytes 3145760 | tf_op jit(solution)/shard_map/all_to_all | solution.py:50
  221.2 61.9 %reshape.101 = bf16[4096,1,6,8,8]{4,3,2,1,0:T(8,128)(2,1)} reshape(bf16[16,2,49152]{2,1,0:T(2,128)(2,1)S(1)} %all-to-all-done.1) | data formatting | bytes 6291456
  283.1 38.4 %copy.48 = bf16[8,16,256,8,1,6]{2,1,3,5,0,4:T(8,128)(2,1)S(1)} copy(bf16[8,16,256,8,1,6]{3,0,5,2,1,4:T(8,128)(2,1)} %bitcast.30) | data formatting | bytes 6291456 | tf_op jit(solution)/shard_map/all_to_all | solution.py:50
  321.5 1.8 copy.41
  323.3 0.2 slice_bitcast_fusion
  323.5 0.2 copy.42
  323.7 2.4 gather_fusion
  326.1 0.0 copy-start
  326.1 2.1 select_bitcast_fusion
  328.2 0.0 copy-done
  328.2 1.5 abs_reduce_fusion
  329.7 0.1 slice_bitcast_fusion.1
  329.8 0.3 slice.39
  330.1 0.9 copy.45
  331.0 0.9 copy.46
  331.9 2.5 copy.43
  334.4 0.1 copy.44
  334.5 19.7 %all_gather.3 = f32[16,8,768]{2,1,0:T(8,128)S(1)} all-gather(f32[1,8,768]{2,1,0:T(8,128)S(1)} %bitcast.39), channel_id=1, replica_groups=mesh['dev'=8,'ma'=16] {'ma'}, dimensions={0}, use_global_device_ids=true | all-gather | bytes 417792 | tf_op jit(solution)/shard_map/all_gather | solution.py:12
  354.3 0.6 reduce_max.19
  (4 shorter events, 0.1 us)
Async XLA Ops:
  173.1 6.0 %copy-start.1 = (s32[128]{0:T(128)S(1)}, s32[128]{0:T(128)}, u32[]{:S(2)}) copy-start(s32[128]{0:T(128)} %param.5) | copy-start | bytes 1540
  173.1 48.1 %all-to-all-start.1 = ((bf16[16,2,49152]{2,1,0:T(2,128)(2,1)}), bf16[16,2,49152]{2,1,0:T(2,128)(2,1)S(1)}, u32[]{:S(2)}, u32[]{:S(2)}) async-start(bf16[16,2,49152]{2,1,0:T(2,128)(2,1)} %reshape.100), calls=%async_computation.1 | async-start | bytes 6291456 | tf_op jit(solution)/shard_map/all_to_all | solution.py:50
  326.1 2.1 copy-start
where the time goes:
time: 356 us; the launch traced here: 355 us
  local copies, waits for them, and re-layouts  220 us (62%)
  blocking collectives  81.1 us (23%)
  waiting for transfers between devices  42.1 us (12%)
  starting transfers between devices  6.01 us (2%)
  other arithmetic  4.59 us (1%)
    unnamed x9, local copies, waits for them, and re-layouts  124 us
    all_to_all x1, blocking collectives, shards(): lax.all_to_all(prepared, 'dev', split_axis=first_split, concat_axis=first...  61.3 us
    all_to_all x1, local copies, waits for them, and re-layouts, shards(): lax.all_to_all(prepared, 'dev', split_axis=first_split, concat_axis=first...  47.9 us
    all_to_all x1, waiting for transfers between devices, shards(): lax.all_to_all(grouped, 'ma', split_axis=second_split, concat_axis=second...  42.1 us
    all_to_all x2, local copies, waits for them, and re-layouts, shards(): lax.all_to_all(grouped, 'ma', split_axis=second_split, concat_axis=second...  40.2 us
    all_gather x1, blocking collectives, over_pieces(): return lax.all_gather(array, axis).max(0)  19.7 us
  transfers between devices with their start and end apart: 1, of which 1 were waited for; matrix products, arithmetic and copies ran while one was open for 0% of the time, Pallas kernels for 0%

commit v1 on v0

v1 whole, which is shorter than its diff:
```python
import jax
import jax.numpy as jnp
from jax import lax
from jax.experimental import pallas as pl
from jax.experimental.pallas import tpu as pltpu
from jax.sharding import PartitionSpec as P

LAYERS = 8
CHUNKS = 16
FEATS = 256
COLS = 384
PIECE = 48
EARLY = 6
LAG_SWAP, LAG_X, LAG_Z, LAG_F = 3, 4, 6, 8
MESH = pl.DeviceIdType.MESH


def sort_matrix(pm_ref):
    row = lax.broadcasted_iota(jnp.int32, (COLS, 128), 0)
    lane = lax.broadcasted_iota(jnp.int32, (COLS, 128), 1)
    g = (row * 1366) >> 16
    rest = row - g * PIECE
    s, dd = rest >> 3, rest & 7
    head = jnp.where(s < 4, g * 4 + s, 32 + (s - 4) * 8 + g)
    column = dd * PIECE + head
    for block in range(COLS // 128):
        pm_ref[:, block * 128 : (block + 1) * 128] = jnp.where(column == lane + block * 128, 1.0, 0.0).astype(jnp.bfloat16)


def order_matrix(rot_ref, rm_ref, zl):
    spread = jnp.broadcast_to(rot_ref[0:1, :], (128, 128))
    turned = jnp.transpose(spread)
    plain = lax.broadcasted_iota(jnp.int32, (128, 128), 0)
    lane = lax.broadcasted_iota(jnp.int32, (128, 128), 1)
    for s in range(6):
        stored = turned if s < 5 else plain
        piece = stored >> 3
        half = piece >> 3
        slot = jnp.where(zl == 1, half, 1 - half)
        column = slot * COLS + (piece & 7) * PIECE + s * 8 + (stored & 7)
        for block in range(2 * COLS // 128):
            rm_ref[s * 128 : (s + 1) * 128, block * 128 : (block + 1) * 128] = jnp.where(
                column == lane + block * 128, 1.0, 0.0
            ).astype(jnp.bfloat16)


def kernel(
    rot_ref, gain_ref, w_ref, q_ref, k_ref, v_ref, peak_ref,
    xb, sb, yb, gb, ob, pk, pm, rm,
    in_sem, swap_sem, y_sem, x_sem, z_sem, swap_out, y_out, x_out, z_out, o_sem, pk_sem, pk_out,
):
    dev, ma = lax.axis_index("dev"), lax.axis_index("ma")
    zh, y = dev // 4, dev % 4
    zl, x, c = ma // 8, (ma // 2) % 4, ma % 2
    z = zh * 2 + zl
    mid = (z == 1) | (z == 2)
    end = (z == 0) | (z == 3)

    def at(x_, y_, z_, c_):
        return {"dev": (z_ // 2) * 4 + y_, "ma": (z_ % 2) * 8 + x_ * 2 + c_}

    def send(src, dst, out_sem, in_sem_, device):
        pltpu.make_async_remote_copy(src, dst, out_sem, in_sem_, device_id=device, device_id_type=MESH).start()

    def done(ref, sem):
        pltpu.make_async_copy(ref, ref, sem).wait()

    def load(t):
        return pltpu.make_async_copy(w_ref.at[t // 2, pl.ds((t % 2) * FEATS, FEATS), :], xb.at[t], in_sem.at[t])

    for t in range(CHUNKS):
        load(t).start()

    barrier = pltpu.get_barrier_semaphore()
    for step in range(1, 4):
        pl.semaphore_signal(barrier, inc=1, device_id=at(x, (y + step) % 4, z, c), device_id_type=MESH)
    for step in range(1, 16):
        pl.semaphore_signal(barrier, inc=1, device_id={"dev": dev, "ma": (ma + step) % 16}, device_id_type=MESH)
    pl.semaphore_signal(barrier, inc=1, device_id=at(x, y, 3 - z, c), device_id_type=MESH)

    sort_matrix(pm)
    order_matrix(rot_ref, rm, zl)
    pl.semaphore_wait(barrier, 19)

    def along_y(t, q):
        pltpu.make_async_copy(sb.at[t, q, y], yb.at[t, q, y], y_sem.at[t * 2 + q]).start()
        for step in (2, 1, 3):
            far = (y + step) % 4
            send(sb.at[t, q, far], yb.at[t, q, y], y_out.at[t], y_sem.at[t * 2 + q], at(x, far, z, c))

    def sort(t):
        load(t).wait()
        for half in range(2):
            rows = lax.dot_general(
                pm[half * 192 : (half + 1) * 192, :], xb[t], (((1,), (1,)), ((), ())), preferred_element_type=jnp.float32
            )
            place = jnp.where(zh == half, 0, jnp.where(mid, 1, 2))
            sb[t, place] = rows.astype(jnp.bfloat16).reshape(4, PIECE, FEATS)

    def first_sends(t):
        @pl.when(end)
        def _():
            send(sb.at[t, 2], sb.at[t, 1], swap_out.at[t], swap_sem.at[t], at(x, y, 3 - z, c))

        along_y(t, 0)

        @pl.when(mid)
        def _():
            along_y(t, 1)

    def swapped(t):
        @pl.when(end)
        def _():
            done(sb.at[t, 1], swap_sem.at[t])
            along_y(t, 1)

    def along_x(t):
        layer, core = t // 2, t % 2
        for q in range(2):
            done(yb.at[t, q], y_sem.at[t * 2 + q])
            slot = jnp.where(end, 1, 2) if q == 0 else 3
            place = gb.at[layer, slot, x * 2 + c]
            for step in (2, 1, 3):
                far = (x + step) % 4
                send(yb.at[t, q, far], place, x_out.at[t], x_sem.at[layer * 2 + q], at(far, y, z, core))

            @pl.when(core != c)
            def _():
                send(yb.at[t, q, x], place, x_out.at[t], x_sem.at[layer * 2 + q], at(x, y, z, 1 - c))

            @pl.when(core == c)
            def _():
                pltpu.make_async_copy(yb.at[t, q, x], place, x_sem.at[layer * 2 + q]).start()

    def along_z(layer):
        done(gb.at[layer, 2], x_sem.at[layer * 2])

        @pl.when(mid)
        def _():
            send(gb.at[layer, 2], gb.at[layer, 0], z_out.at[layer], z_sem.at[layer * 2], at(x, y, 3 * (z // 2), c))

        done(gb.at[layer, 3], x_sem.at[layer * 2 + 1])
        slot = jnp.where(end, 1, 0)
        send(gb.at[layer, 3], gb.at[layer, slot], z_out.at[layer], z_sem.at[layer * 2 + slot], at(x, y, 1 + z % 2, c))

    def send_peaks(part, first, count):
        for step in range(1, 16):
            block = pk.at[ma, pl.ds(first, count)]
            send(block, block, pk_out.at[part], pk_sem.at[part], {"dev": dev, "ma": (ma + step) % 16})

    def finish(layer):
        done(gb.at[layer, 0], z_sem.at[layer * 2])

        @pl.when(mid)
        def _():
            done(gb.at[layer, 1], z_sem.at[layer * 2 + 1])

        arrived = gb[layer, 0:2].reshape(2 * COLS, FEATS)
        gain = gain_ref[pl.ds(layer, 1), :]
        for s in range(6):
            rows = jnp.dot(rm[s * 128 : (s + 1) * 128, :], arrived, preferred_element_type=jnp.float32) * gain
            ob[layer, s * 128 : (s + 1) * 128, :] = rows.astype(jnp.bfloat16)
            size = jnp.abs(rows)
            size = jnp.transpose(jnp.maximum(size[:, :128], size[:, 128:]))
            top = jnp.max(size, axis=0, keepdims=True)
            pk[ma, layer, s : s + 1, :] = top.astype(jnp.bfloat16).astype(jnp.float32)
        pltpu.make_async_copy(ob.at[layer, pl.ds(0, 512)], q_ref.at[layer], o_sem.at[layer]).start()
        pltpu.make_async_copy(ob.at[layer, pl.ds(512, 128)], k_ref.at[layer], o_sem.at[layer]).start()
        pltpu.make_async_copy(ob.at[layer, pl.ds(640, 128)], v_ref.at[layer], o_sem.at[layer]).start()

        @pl.when(layer == EARLY - 1)
        def _():
            send_peaks(0, 0, EARLY)

        @pl.when(layer == LAYERS - 1)
        def _():
            send_peaks(1, EARLY, LAYERS - EARLY)

    def turn(i, carry):
        def during(lag, stage):
            t = i - lag

            @pl.when((t >= 0) & (t < CHUNKS))
            def _():
                stage(t)

        def mine(stage):
            def run(t):
                @pl.when(t % 2 == c)
                def _():
                    stage(t // 2)

            return run

        during(0, sort)
        during(1, first_sends)
        during(LAG_SWAP, swapped)
        during(LAG_X, along_x)
        during(LAG_Z, mine(along_z))
        during(LAG_F, mine(finish))
        return carry

    lax.fori_loop(0, CHUNKS + LAG_F, turn, 0)

    def close(t, carry):
        done(sb.at[t, 0:2, 0:3], y_out.at[t])

        @pl.when(end)
        def _():
            done(sb.at[t, 2], swap_out.at[t])

        @pl.when(t % 2 == c)
        def _():
            done(yb.at[t, :, 0:3], x_out.at[t])

        @pl.when(t % 2 != c)
        def _():
            done(yb.at[t], x_out.at[t])

        return carry

    lax.fori_loop(0, CHUNKS, close, 0)

    def close_layer(layer, carry):
        @pl.when(end)
        def _():
            done(gb.at[layer, 3], z_out.at[layer])

        @pl.when(mid)
        def _():
            done(gb.at[layer, 2:4], z_out.at[layer])

        done(ob.at[layer], o_sem.at[layer])
        return carry

    lax.fori_loop(0, LAYERS, close_layer, 0)

    for part, count in ((0, EARLY), (1, LAYERS - EARLY)):
        done(pk.at[0:15, 0:count], pk_sem.at[part])
        done(pk.at[0:15, 0:count], pk_out.at[part])
    for s in range(6):
        peak_ref[:, s * 128 : (s + 1) * 128] = jnp.max(pk[:, :, s, :], axis=0)


def shards(joined_weight, norm_gain, rotary_order):
    dma = pltpu.SemaphoreType.DMA
    bf16 = jnp.bfloat16
    return pl.pallas_call(
        kernel,
        name="relayout",
        out_shape=(
            jax.ShapeDtypeStruct((LAYERS, 512, FEATS), bf16),
            jax.ShapeDtypeStruct((LAYERS, 128, FEATS), bf16),
            jax.ShapeDtypeStruct((LAYERS, 128, FEATS), bf16),
            jax.ShapeDtypeStruct((LAYERS, 768), jnp.float32),
        ),
        in_specs=[
            pl.BlockSpec(memory_space=pltpu.VMEM),
            pl.BlockSpec(memory_space=pltpu.VMEM),
            pl.BlockSpec(memory_space=pl.ANY),
        ],
        out_specs=(
            pl.BlockSpec(memory_space=pl.ANY),
            pl.BlockSpec(memory_space=pl.ANY),
            pl.BlockSpec(memory_space=pl.ANY),
            pl.BlockSpec(memory_space=pltpu.VMEM),
        ),
        scratch_shapes=[
            pltpu.VMEM((CHUNKS, FEATS, COLS), bf16),
            pltpu.VMEM((CHUNKS, 3, 4, PIECE, FEATS), bf16),
            pltpu.VMEM((CHUNKS, 2, 4, PIECE, FEATS), bf16),
            pltpu.VMEM((LAYERS, 4, 8, PIECE, FEATS), bf16),
            pltpu.VMEM((LAYERS, 768, FEATS), bf16),
            pltpu.VMEM((16, LAYERS, 8, 128), jnp.float32),
            pltpu.VMEM((COLS, COLS), bf16),
            pltpu.VMEM((768, 768), bf16),
            dma((CHUNKS,)),
            dma((CHUNKS,)),
            dma((CHUNKS * 2,)),
            dma((LAYERS * 2,)),
            dma((LAYERS * 2,)),
            dma((CHUNKS,)),
            dma((CHUNKS,)),
            dma((CHUNKS,)),
            dma((LAYERS,)),
            dma((LAYERS,)),
            dma((2,)),
            dma((2,)),
        ],
        compiler_params=pltpu.CompilerParams(collective_id=0, has_side_effects=True, vmem_limit_bytes=40 * 2**20),
    )(rotary_order.reshape(1, 128), norm_gain, joined_weight)


def solution(mesh):
    placed = (P(None, "dev", "ma"), P(None, "ma"), P())
    tiles = P(None, "dev", "ma")
    return jax.shard_map(shards, mesh=mesh, in_specs=placed, out_specs=(tiles, tiles, tiles, P(None, "dev")), check_vma=False)
```

time: 356 us -> 92.1 us (0.26)
  local copies, waits for them, and re-layouts: 220 us -> 6.75 us
  Pallas kernels: 0 us -> 84.5 us
  blocking collectives: 81.1 us -> 0 us
  waiting for transfers between devices: 42.1 us -> 0 us
  starting transfers between devices: 6.01 us -> 0 us
  other arithmetic: 4.59 us -> 0 us
    unnamed x9 -> x10, local copies, waits for them, and re-layouts: 124 us -> 6.75 us
    all_to_all x3 -> x0, local copies, waits for them, and re-layouts: 88 us -> none  [the longest x1 47.9 us: shards(): lax.all_to_all(prepared, 'dev', split_axis=first_split, concat_axis=first...]
    pallas_call x0 -> x1, Pallas kernels: none -> 84.5 us  [shards(): pl.pallas_call(kernel, name='relayout', out_shape=(jax.ShapeDtypeStruct((...]
    all_to_all x1 -> x0, blocking collectives: 61.3 us -> none  [shards(): lax.all_to_all(prepared, 'dev', split_axis=first_split, concat_axis=first...]
    all_to_all x1 -> x0, waiting for transfers between devices: 42.1 us -> none  [shards(): lax.all_to_all(grouped, 'ma', split_axis=second_split, concat_axis=second...]
    all_gather x1 -> x0, blocking collectives: 19.7 us -> none  [over_pieces(): return lax.all_gather(array, axis).max(0)]
    all_to_all x1 -> x0, starting transfers between devices: 6.01 us -> none  [shards(): lax.all_to_all(grouped, 'ma', split_axis=second_split, concat_axis=second...]
    slice x7 -> x0, local copies, waits for them, and re-layouts: 4.64 us -> none  [the longest x2 2.82 us: finish_tiles(): query_rows = scaled[:, :, :GROUP].reshape(layer_count, -1, column_count)]
  transfers between devices with their start and end apart: 1 -> 0, of which waited for: 1 -> 0; matrix products, arithmetic and copies ran while one was open for 0% -> 0% of each run, Pallas kernels for 0% -> 0%
where the time goes in v1:
time: 92.1 us; the launch traced here: 91.9 us
  Pallas kernels  84.5 us (92%)
  local copies, waits for them, and re-layouts  6.75 us (7%)
    pallas_call x1, Pallas kernels, shards(): pl.pallas_call(kernel, name='relayout', out_shape=(jax.ShapeDtypeStruct((...  84.5 us
    unnamed x10, local copies, waits for them, and re-layouts  6.75 us

profile of v1, /device:TPU:1, one launch (start us, length us, event | category | flops | bytes accessed | tf_op | source)
XLA Modules:
  0.0 91.9 jit_solution(7259794940028475037)
XLA Ops:
  0.6 0.0 copy-start
  0.6 1.9 %copy-done = bf16[8,512,384]{2,1,0:T(8,128)(2,1)S(1)} copy-done((bf16[8,512,384]{2,1,0:T(8,128)(2,1)S(1)}, bf16[8,512,384]{2,1,0:T(8,128)(2,1)}, u32[]{:S(2)}) %copy-start) | copy-done | bytes 3145752
  2.5 0.0 copy-start.1
  2.5 0.7 copy-done.1
  3.2 0.0 copy-start.2
  3.2 0.7 copy-done.2
  3.9 84.5 %relayout.1 = (bf16[8,512,256]{2,1,0:T(8,128)(2,1)S(1)}, bf16[8,128,256]{2,1,0:T(8,128)(2,1)S(1)}, bf16[8,128,256]{2,1,0:T(8,128)(2,1)S(1)}, f32[8,768]{1,0:T(8,128)S(1)}) custom-call(s32[1,128]{1,0:T(1,128)S(1)} %bitcast.1, f32[8,256]{1,0:T(8,128)S(1)} %copy-done.1, bf16[8,512,384]{2,1,0:T(8,128)(2,1)S(1)} %copy-done), custom_call_target="tpu_custom_call" | custom-call | tf_op jit(solution)/shard_map/relayout/pallas_call | solution.py:248
  88.4 1.3 %copy.11 = bf16[8,512,256]{2,1,0:T(8,128)(2,1)} copy(bf16[8,512,256]{2,1,0:T(8,128)(2,1)S(1)} %get-tuple-element.8) | data formatting | bytes 4194304
  89.7 0.8 copy.12
  90.5 0.8 copy.13
  91.3 0.6 copy.14
Async XLA Ops:
  0.6 1.9 %copy-start = (bf16[8,512,384]{2,1,0:T(8,128)(2,1)S(1)}, bf16[8,512,384]{2,1,0:T(8,128)(2,1)}, u32[]{:S(2)}) copy-start(bf16[8,512,384]{2,1,0:T(8,128)(2,1)} %w_ref.1) | copy-start | bytes 9437188
  2.5 0.7 copy-start.1
  3.2 0.7 copy-start.2

commit v2 on v1

v2 whole, which is shorter than its diff:
```python
import jax
import jax.numpy as jnp
from jax import lax
from jax.experimental import pallas as pl
from jax.experimental.pallas import tpu as pltpu
from jax.sharding import PartitionSpec as P

LAYERS = 8
CHUNKS = 16
FEATS = 256
COLS = 384
PIECE = 48
PAIRS = 3
AHEAD = 4
SKEW = 3
STEPS = 2 * CHUNKS
LAG_X, LAG_Z, LAG_F = 4, 8, 12
PEAKS_FROM, PEAKS_SEND, PEAKS_GROUP, PEAKS_SPREAD, PEAKS_LAST = 8, 24, 28, 30, 36
MESH = pl.DeviceIdType.MESH


def sort_matrix(pm_ref):
    row = lax.broadcasted_iota(jnp.int32, (COLS, 128), 0)
    lane = lax.broadcasted_iota(jnp.int32, (COLS, 128), 1)
    g = (row * 1366) >> 16
    rest = row - g * PIECE
    s, dd = rest >> 3, rest & 7
    head = jnp.where(s < 4, g * 4 + s, 32 + (s - 4) * 8 + g)
    column = dd * PIECE + head
    for block in range(COLS // 128):
        pm_ref[:, block * 128 : (block + 1) * 128] = jnp.where(column == lane + block * 128, 1.0, 0.0).astype(jnp.bfloat16)


def order_matrix(rot_ref, rm_ref, zl):
    turned = jnp.transpose(jnp.broadcast_to(rot_ref[0:1, :], (128, 128)))
    plain = lax.broadcasted_iota(jnp.int32, (128, 128), 0)
    lane = lax.broadcasted_iota(jnp.int32, (128, 128), 1)

    def hot(stored, s2, block):
        piece = stored >> 3
        half = piece >> 3
        slot = jnp.where(zl == 1, half, 1 - half)
        column = slot * 128 + (piece & 7) * 16 + s2 * 8 + (stored & 7)
        return jnp.where(column == lane + block * 128, 1.0, 0.0).astype(jnp.bfloat16)

    for block in range(2):
        lanes = slice(block * 128, (block + 1) * 128)
        key = hot(turned, 0, block)
        rm_ref[0, 0:128, lanes] = key
        rm_ref[1, 0:128, lanes] = key
        rm_ref[0, 128:256, lanes] = hot(turned, 1, block)
        rm_ref[1, 128:256, lanes] = hot(plain, 1, block)


def kernel(
    rot_ref, gain_ref, w_ref, out_ref, peak_ref,
    rv, gv, gs, xb, sb, yb, gb, ob, pt, pk1, pk2, pm, rm,
    in_sem, rot_sem, gain_sem, gs_sem, gs_out, swap_sem, y_sem, x_sem, z_sem, swap_out, y_out, x_out, z_out, o_sem,
    pk1_sem, pk1_out, pk2_sem, pk2_out,
):
    dev, ma = lax.axis_index("dev"), lax.axis_index("ma")
    zh, y = dev // 4, dev % 4
    zl, x, c = ma // 8, (ma // 2) % 4, ma % 2
    z = zh * 2 + zl
    inner = (z == 1) | (z == 2)
    outer = (z == 0) | (z == 3)
    opposite = {"dev": (1 - zh) * 4 + y, "ma": (1 - zl) * 8 + x * 2 + c}

    def at(x_, y_, z_, c_):
        return {"dev": (z_ // 2) * 4 + y_, "ma": (z_ % 2) * 8 + x_ * 2 + c_}

    def send(src, dst, out_sem, in_sem_, device):
        pltpu.make_async_remote_copy(src, dst, out_sem, in_sem_, device_id=device, device_id_type=MESH).start()

    def done(ref, sem):
        pltpu.make_async_copy(ref, ref, sem).wait()

    def load(t):
        return pltpu.make_async_copy(w_ref.at[t // 2, pl.ds((t % 2) * FEATS, FEATS), :], xb.at[t], in_sem.at[t])

    load_rot = pltpu.make_async_copy(rot_ref, rv, rot_sem)
    load_gain = pltpu.make_async_copy(gain_ref, gv, gain_sem)

    for t in range(CHUNKS):
        load(t).start()
    load_rot.start()
    load_gain.start()

    barrier = pltpu.get_barrier_semaphore()
    for step in range(1, 16):
        pl.semaphore_signal(barrier, inc=1, device_id={"dev": dev, "ma": (ma + step) % 16}, device_id_type=MESH)
    for step in range(1, 8):
        pl.semaphore_signal(barrier, inc=1, device_id={"dev": (dev + step) % 8, "ma": ma}, device_id_type=MESH)
    pl.semaphore_signal(barrier, inc=1, device_id=opposite, device_id_type=MESH)

    def place(half):
        return jnp.where(zh == half, 0, jnp.where(inner, 1, 2))

    def sort(t):
        load(t).wait()
        rows = lax.dot_general(pm[...], xb[t], (((1,), (1,)), ((), ())), preferred_element_type=jnp.float32)
        rows = rows.astype(jnp.bfloat16).reshape(2, 4, PAIRS, 16, FEATS)
        sb[t, place(0)] = rows[0]
        sb[t, place(1)] = rows[1]

    def swap(t):
        @pl.when(outer)
        def _():
            send(sb.at[t, 2], sb.at[t, 1], swap_out.at[t], swap_sem.at[t], opposite)

    sort_matrix(pm)
    for t in range(AHEAD):
        sort(t)
    load_gain.wait()
    load_rot.wait()
    pl.semaphore_wait(barrier, 23)
    for t in range(AHEAD):
        swap(t)

    def along_y(t, q):
        @pl.when(outer & (q == 1))
        def _():
            done(sb.at[t, 1], swap_sem.at[t])

        pltpu.make_async_copy(sb.at[t, q, y], yb.at[t, q, y], y_sem.at[t * 2 + q]).start()
        for step in (2, 1, 3):
            far = (y + step) % 4
            send(sb.at[t, q, far], yb.at[t, q, y], y_out.at[t], y_sem.at[t * 2 + q], at(x, far, z, c))

    def along_x(t, q):
        layer, core = t // 2, t % 2
        arrived, sem = x_out.at[t], x_sem.at[layer * 2 + q]
        done(yb.at[t, q], y_sem.at[t * 2 + q])
        slot = jnp.where(q == 1, 3, jnp.where(outer, 1, 2))
        target = gb.at[layer, :, slot, x * 2 + c]
        for step in (2, 1, 3):
            far = (x + step) % 4
            send(yb.at[t, q, far], target, arrived, sem, at(far, y, z, core))

        @pl.when(core != c)
        def _():
            send(yb.at[t, q, x], target, arrived, sem, at(x, y, z, 1 - c))

        @pl.when(core == c)
        def _():
            pltpu.make_async_copy(yb.at[t, q, x], target, sem).start()

    def along_z(t, q):
        layer = t // 2

        @pl.when(t % 2 == c)
        def _():
            done(gb.at[layer, :, 2 + q], x_sem.at[layer * 2 + q])

            @pl.when(inner | (q == 1))
            def _():
                slot = jnp.where(outer, 1, 0)
                to = jnp.where(q == 1, 1 + z % 2, 3 * (z // 2))
                target = gb.at[layer, :, slot]
                send(gb.at[layer, :, 2 + q], target, z_out.at[layer], z_sem.at[layer * 2 + slot], at(x, y, to, c))

    def finish(t, q):
        layer = t // 2

        @pl.when((t % 2 == c) & ((outer & (q == 0)) | (inner & (q == 1))))
        def _():
            done(gb.at[layer, :, 0], z_sem.at[layer * 2])

            @pl.when(inner)
            def _():
                done(gb.at[layer, :, 1], z_sem.at[layer * 2 + 1])

            gain = gv[pl.ds(layer, 1), :]
            for pair in range(PAIRS):
                arrived = gb[layer, pair, 0:2].reshape(256, FEATS)
                rows = jnp.dot(rm[pair // 2], arrived, preferred_element_type=jnp.float32) * gain
                ob[layer, pair * 256 : (pair + 1) * 256, :] = rows.astype(jnp.bfloat16)
            pltpu.make_async_copy(ob.at[layer], out_ref.at[layer], o_sem.at[layer]).start()

    def share_gain():
        @pl.when(ma // 2 == dev)
        def _():
            block = ma % 2
            pltpu.make_async_copy(gv, gs.at[block], gs_sem.at[block]).start()
            for step in range(1, 16):
                send(gv, gs.at[block], gs_out, gs_sem.at[block], {"dev": dev, "ma": (ma + step) % 16})

    def peaks(layer):
        @pl.when(layer == 0)
        def _():
            done(gs.at[0], gs_sem.at[0])
            done(gs.at[1], gs_sem.at[1])

        lane = lax.broadcasted_iota(jnp.int32, (192, 128), 1)
        for half in range(2):
            size = None
            for core in range(2):
                rows = sb[layer * 2 + core, place(half)].reshape(192, FEATS).astype(jnp.float32)
                rows = jnp.abs(rows * gs[core, pl.ds(layer, 1), :])
                rows = jnp.maximum(rows[:, :128], rows[:, 128:])
                size = rows if size is None else jnp.maximum(size, rows)
            top = jnp.max(size, axis=1, keepdims=True)
            part = slice(half * 192, (half + 1) * 192)
            pt[part, :] = jnp.where(lane == layer, top, pt[part, :])

        @pl.when(layer == LAYERS - 1)
        def _():
            for block in range(3):
                lanes = slice(block * 128, (block + 1) * 128)
                pk1[dev, :, lanes] = jnp.transpose(pt[lanes, :])[0:LAYERS, :].astype(jnp.bfloat16).astype(jnp.float32)

    def send_peaks():
        for step in range(1, 8):
            send(pk1.at[dev], pk1.at[dev], pk1_out, pk1_sem, {"dev": (dev + step) % 8, "ma": ma})

    def group_peaks():
        done(pk1.at[0:7], pk1_sem)
        top = jnp.max(pk1[...], axis=0).astype(jnp.bfloat16)
        row = lax.broadcasted_iota(jnp.int32, (COLS, 128), 0)
        lane = lax.broadcasted_iota(jnp.int32, (COLS, 128), 1)
        pick = jnp.where((row - dev * PIECE == lane) & (lane < PIECE), 1.0, 0.0).astype(jnp.bfloat16)
        pk2[ma] = jnp.dot(top, pick, preferred_element_type=jnp.float32)

    def spread_peaks():
        for step in range(1, 16):
            send(pk2.at[ma], pk2.at[ma], pk2_out, pk2_sem, {"dev": dev, "ma": (ma + step) % 16})

    def last_peaks():
        done(pk2.at[0:15], pk2_sem)
        lane = lax.broadcasted_iota(jnp.int32, (LAYERS, 128), 1)
        for pair in range(PAIRS):
            halves = []
            for half in range(2):
                line = jnp.zeros((LAYERS, 128), jnp.float32)
                for piece in range(8):
                    shift = (piece - pair) * 16 % 128
                    part = pk2[half * 8 + piece]
                    part = pltpu.roll(part, shift, 1) if shift else part
                    line = jnp.where((lane >= piece * 16) & (lane < piece * 16 + 16), part, line)
                halves.append(line)
            low = jnp.where(zl == 1, halves[0], halves[1])
            high = jnp.where(zl == 1, halves[1], halves[0])
            line = jnp.concatenate([low, high], axis=1).astype(jnp.bfloat16)
            peak_ref[:, pair * 256 : (pair + 1) * 256] = lax.dot_general(
                line, rm[pair // 2], (((1,), (1,)), ((), ())), preferred_element_type=jnp.float32
            )

    def order(u):
        later = u - SKEW
        even = later % 2 == 0
        t = jnp.where(u < SKEW, u, jnp.where(u >= STEPS - SKEW, u - CHUNKS, jnp.where(even, later // 2, SKEW + later // 2)))
        q = jnp.where(u < SKEW, 0, jnp.where(u >= STEPS - SKEW, 1, jnp.where(even, 1, 0)))
        return t, q

    def turn(i, carry):
        def during(lag, stage):
            @pl.when((i >= lag) & (i < STEPS + lag))
            def _():
                stage(*order(i - lag))

        def keep_sorted(t, q):
            @pl.when((q == 0) & (t + AHEAD < CHUNKS))
            def _():
                sort(t + AHEAD)

            @pl.when((q == 0) & (t > 0) & (t + AHEAD - 1 < CHUNKS))
            def _():
                swap(t + AHEAD - 1)

        during(0, along_y)
        during(LAG_X, along_x)
        during(LAG_Z, along_z)
        during(0, keep_sorted)
        during(LAG_F, finish)

        @pl.when((i >= PEAKS_FROM) & (i < PEAKS_FROM + 2 * LAYERS) & (i % 2 == 0))
        def _():
            peaks((i - PEAKS_FROM) // 2)

        pl.when(i == PEAKS_SEND)(send_peaks)
        pl.when(i == PEAKS_GROUP)(group_peaks)
        pl.when(i == PEAKS_SPREAD)(spread_peaks)
        pl.when(i == PEAKS_LAST)(last_peaks)

        @pl.when(i == 0)
        def _():
            share_gain()
            order_matrix(rv, rm, zl)

        return carry

    lax.fori_loop(0, STEPS + LAG_F, turn, 0)

    def close(t, carry):
        done(sb.at[t, 0:2, 0:3], y_out.at[t])

        @pl.when(outer)
        def _():
            done(sb.at[t, 2], swap_out.at[t])

        @pl.when(t % 2 == c)
        def _():
            done(yb.at[t, :, 0:3], x_out.at[t])

        @pl.when(t % 2 != c)
        def _():
            done(yb.at[t], x_out.at[t])

        return carry

    lax.fori_loop(0, CHUNKS, close, 0)

    def close_layer(layer, carry):
        @pl.when(outer)
        def _():
            done(gb.at[layer, :, 3], z_out.at[layer])

        @pl.when(inner)
        def _():
            done(gb.at[layer, :, 2:4], z_out.at[layer])

        done(ob.at[layer], o_sem.at[layer])
        return carry

    lax.fori_loop(0, LAYERS, close_layer, 0)

    @pl.when(ma // 2 == dev)
    def _():
        done(gs.at[0:15], gs_out)

    done(pk1.at[0:7], pk1_out)
    done(pk2.at[0:15], pk2_out)


def write_out(tiles_ref, peak_ref, q_ref, k_ref, v_ref, row_ref, sem):
    copies = [
        pltpu.make_async_copy(tiles_ref.at[:, pl.ds(0, 512)], q_ref, sem.at[0]),
        pltpu.make_async_copy(tiles_ref.at[:, pl.ds(512, 128)], k_ref, sem.at[1]),
        pltpu.make_async_copy(tiles_ref.at[:, pl.ds(640, 128)], v_ref, sem.at[2]),
        pltpu.make_async_copy(peak_ref, row_ref, sem.at[3]),
    ]
    for copy in copies:
        copy.start()
    for copy in copies:
        copy.wait()


def shards(joined_weight, norm_gain, rotary_order):
    dma = pltpu.SemaphoreType.DMA
    bf16, f32 = jnp.bfloat16, jnp.float32
    hbm = pl.BlockSpec(memory_space=pltpu.HBM)
    anywhere = pl.BlockSpec(memory_space=pl.ANY)
    tiles, peak = pl.pallas_call(
        kernel,
        name="relayout",
        out_shape=(jax.ShapeDtypeStruct((LAYERS, 768, FEATS), bf16), jax.ShapeDtypeStruct((LAYERS, 768), f32)),
        in_specs=[hbm, hbm, hbm],
        out_specs=(anywhere, pl.BlockSpec(memory_space=pltpu.VMEM)),
        scratch_shapes=[
            pltpu.VMEM((1, 128), jnp.int32),
            pltpu.VMEM((LAYERS, FEATS), f32),
            pltpu.VMEM((15, LAYERS, FEATS), f32),
            pltpu.VMEM((CHUNKS, FEATS, COLS), bf16),
            pltpu.VMEM((CHUNKS, 3, 4, PAIRS, 16, FEATS), bf16),
            pltpu.VMEM((CHUNKS, 2, 4, PAIRS, 16, FEATS), bf16),
            pltpu.VMEM((LAYERS, PAIRS, 4, 8, 16, FEATS), bf16),
            pltpu.VMEM((LAYERS, 768, FEATS), bf16),
            pltpu.VMEM((COLS, 128), f32),
            pltpu.VMEM((8, LAYERS, COLS), f32),
            pltpu.VMEM((16, LAYERS, 128), f32),
            pltpu.VMEM((COLS, COLS), bf16),
            pltpu.VMEM((2, 256, 256), bf16),
            dma((CHUNKS,)),
            dma,
            dma,
            dma((2,)),
            dma,
            dma((CHUNKS,)),
            dma((CHUNKS * 2,)),
            dma((LAYERS * 2,)),
            dma((LAYERS * 2,)),
            dma((CHUNKS,)),
            dma((CHUNKS,)),
            dma((CHUNKS,)),
            dma((LAYERS,)),
            dma((LAYERS,)),
            dma,
            dma,
            dma,
            dma,
        ],
        compiler_params=pltpu.CompilerParams(collective_id=0, has_side_effects=True, vmem_limit_bytes=40 * 2**20),
    )(*(pltpu.with_memory_space_constraint(a, pltpu.HBM) for a in (rotary_order.reshape(1, 128), norm_gain, joined_weight)))
    return pl.pallas_call(
        write_out,
        name="write_out",
        out_shape=(
            jax.ShapeDtypeStruct((LAYERS, 512, FEATS), bf16),
            jax.ShapeDtypeStruct((LAYERS, 128, FEATS), bf16),
            jax.ShapeDtypeStruct((LAYERS, 128, FEATS), bf16),
            jax.ShapeDtypeStruct((LAYERS, 768), f32),
        ),
        in_specs=[anywhere, anywhere],
        out_specs=(hbm, hbm, hbm, hbm),
        scratch_shapes=[dma((4,))],
        compiler_params=pltpu.CompilerParams(vmem_limit_bytes=2**20),
    )(tiles, peak)


def solution(mesh):
    placed = (P(None, "dev", "ma"), P(None, "ma"), P())
    tiles = P(None, "dev", "ma")
    return jax.shard_map(shards, mesh=mesh, in_specs=placed, out_specs=(tiles, tiles, tiles, P(None, "dev")), check_vma=False)
```

time: 92.1 us -> 67.9 us (0.74)
  Pallas kernels: 84.5 us -> 66.7 us
  local copies, waits for them, and re-layouts: 6.75 us -> 0 us
    pallas_call x1, Pallas kernels: 84.5 us -> 65 us  [shards(): pl.pallas_call(kernel, name='relayout', out_shape=(jax.ShapeDtypeStruct((...]
    unnamed x10 -> x0, local copies, waits for them, and re-layouts: 6.75 us -> none
    pallas_call x0 -> x1, Pallas kernels: none -> 1.69 us  [shards(): pl.pallas_call(write_out, name='write_out', out_shape=(jax.ShapeDtypeStru...]
where the time goes in v2:
time: 67.9 us; the launch traced here: 67.4 us
  Pallas kernels  66.7 us (98%)
    pallas_call x1, Pallas kernels, shards(): pl.pallas_call(kernel, name='relayout', out_shape=(jax.ShapeDtypeStruct((...  65 us
    pallas_call x1, Pallas kernels, shards(): pl.pallas_call(write_out, name='write_out', out_shape=(jax.ShapeDtypeStru...  1.69 us

profile of v2, /device:TPU:1, one launch (start us, length us, event | category | flops | bytes accessed | tf_op | source)
XLA Modules:
  0.0 67.4 jit_solution(17242846701766378196)
XLA Ops:
  0.6 65.0 %relayout.1 = (bf16[8,768,256]{2,1,0:T(8,128)(2,1)S(1)}, f32[8,768]{1,0:T(8,128)S(1)}) custom-call(s32[1,128]{1,0:T(1,128)} %bitcast.1, f32[8,256]{1,0:T(8,128)} %gain_ref.1, bf16[8,512,384]{2,1,0:T(8,128)(2,1)} %w_ref.1), custom_call_target="tpu_custom_call" | custom-call | tf_op jit(solution)/shard_map/relayout/pallas_call | solution.py:353
  65.7 1.7 %write_out.1 = (bf16[8,512,256]{2,1,0:T(8,128)(2,1)}, bf16[8,128,256]{2,1,0:T(8,128)(2,1)}, bf16[8,128,256]{2,1,0:T(8,128)(2,1)}, f32[8,768]{1,0:T(8,128)}) custom-call(bf16[8,768,256]{2,1,0:T(8,128)(2,1)S(1)} %get-tuple-element.6.tiles_ref, f32[8,768]{1,0:T(8,128)S(1)} %get-tuple-element.7.peak_ref), custom_call_target="tpu_custom_call" | custom-call | tf_op jit(solution)/shard_map/write_out/pallas_call | solution.py:394

commit v3 on v2

--- a/solution.py
+++ b/solution.py
@@ -11,11 +11,12 @@
 COLS = 384
 PIECE = 48
 PAIRS = 3
-AHEAD = 4
-SKEW = 3
+LATE = 8
+AHEAD = 8
 STEPS = 2 * CHUNKS
-LAG_X, LAG_Z, LAG_F = 4, 8, 12
-PEAKS_FROM, PEAKS_SEND, PEAKS_GROUP, PEAKS_SPREAD, PEAKS_LAST = 8, 24, 28, 30, 36
+Z_LAST, Z_LAST_RELAY, Z_FIRST_RELAY, FINISH_LATE, FINISH = 5, 20, 3, 25, 23
+PEAKS_FROM, PEAKS_SEND, PEAKS_GROUP, PEAKS_SPREAD, PEAKS_LAST = 10, 25, 29, 30, 34
+END = max(FINISH, FINISH_LATE) + 15
 MESH = pl.DeviceIdType.MESH
 
 
@@ -55,7 +56,7 @@
 def kernel(
     rot_ref, gain_ref, w_ref, out_ref, peak_ref,
     rv, gv, gs, xb, sb, yb, gb, ob, pt, pk1, pk2, pm, rm,
-    in_sem, rot_sem, gain_sem, gs_sem, gs_out, swap_sem, y_sem, x_sem, z_sem, swap_out, y_out, x_out, z_out, o_sem,
+    in_sem, rot_sem, gain_sem, gs_sem, gs_out, far_sem, near_sem, y_sem, x_sem, z_sem, first_out, y_out, x_out, z_out, o_sem,
     pk1_sem, pk1_out, pk2_sem, pk2_out,
 ):
     dev, ma = lax.axis_index("dev"), lax.axis_index("ma")
@@ -64,7 +65,8 @@
     z = zh * 2 + zl
     inner = (z == 1) | (z == 2)
     outer = (z == 0) | (z == 3)
-    opposite = {"dev": (1 - zh) * 4 + y, "ma": (1 - zl) * 8 + x * 2 + c}
+    far_z = {"dev": (1 - zh) * 4 + y, "ma": (1 - zl) * 8 + x * 2 + c}
+    near_z = {"dev": dev, "ma": (1 - zl) * 8 + x * 2 + c}
 
     def at(x_, y_, z_, c_):
         return {"dev": (z_ // 2) * 4 + y_, "ma": (z_ % 2) * 8 + x_ * 2 + c_}
@@ -81,8 +83,8 @@
     load_rot = pltpu.make_async_copy(rot_ref, rv, rot_sem)
     load_gain = pltpu.make_async_copy(gain_ref, gv, gain_sem)
 
-    for t in range(CHUNKS):
-        load(t).start()
+    for n in range(CHUNKS):
+        load(n // 2 + (n % 2) * LATE).start()
     load_rot.start()
     load_gain.start()
 
@@ -91,36 +93,42 @@
         pl.semaphore_signal(barrier, inc=1, device_id={"dev": dev, "ma": (ma + step) % 16}, device_id_type=MESH)
     for step in range(1, 8):
         pl.semaphore_signal(barrier, inc=1, device_id={"dev": (dev + step) % 8, "ma": ma}, device_id_type=MESH)
-    pl.semaphore_signal(barrier, inc=1, device_id=opposite, device_id_type=MESH)
-
-    def place(half):
-        return jnp.where(zh == half, 0, jnp.where(inner, 1, 2))
-
-    def sort(t):
+    pl.semaphore_signal(barrier, inc=1, device_id=far_z, device_id_type=MESH)
+
+    def place(t, half):
+        kept = zh == half
+        early = jnp.where(kept, jnp.where(outer, 0, 3), 2)
+        return jnp.where(t < LATE, jnp.where(kept, 0, 1), early)
+
+    def sort(n):
+        t = n // 2 + (n % 2) * LATE
         load(t).wait()
         rows = lax.dot_general(pm[...], xb[t], (((1,), (1,)), ((), ())), preferred_element_type=jnp.float32)
         rows = rows.astype(jnp.bfloat16).reshape(2, 4, PAIRS, 16, FEATS)
-        sb[t, place(0)] = rows[0]
-        sb[t, place(1)] = rows[1]
-
-    def swap(t):
+        sb[t, place(t, 0)] = rows[0]
+        sb[t, place(t, 1)] = rows[1]
+
+    def z_first(t):
+        send(sb.at[t, 2], sb.at[t, jnp.where(outer, 3, 0)], first_out.at[t], far_sem.at[t], far_z)
+
+        @pl.when(inner)
+        def _():
+            send(sb.at[t, 3], sb.at[t, 1], first_out.at[t], near_sem.at[t], near_z)
+
+    def z_first_relay(t):
         @pl.when(outer)
         def _():
-            send(sb.at[t, 2], sb.at[t, 1], swap_out.at[t], swap_sem.at[t], opposite)
-
-    sort_matrix(pm)
-    for t in range(AHEAD):
-        sort(t)
-    load_gain.wait()
-    load_rot.wait()
-    pl.semaphore_wait(barrier, 23)
-    for t in range(AHEAD):
-        swap(t)
+            done(sb.at[t, 3], far_sem.at[t])
+            send(sb.at[t, 3], sb.at[t, 1], first_out.at[t], near_sem.at[t], near_z)
 
     def along_y(t, q):
-        @pl.when(outer & (q == 1))
-        def _():
-            done(sb.at[t, 1], swap_sem.at[t])
+        @pl.when((t >= LATE) & (q == 0) & inner)
+        def _():
+            done(sb.at[t, 0], far_sem.at[t])
+
+        @pl.when((t >= LATE) & (q == 1))
+        def _():
+            done(sb.at[t, 1], near_sem.at[t])
 
         pltpu.make_async_copy(sb.at[t, q, y], yb.at[t, q, y], y_sem.at[t * 2 + q]).start()
         for step in (2, 1, 3):
@@ -129,53 +137,74 @@
 
     def along_x(t, q):
         layer, core = t // 2, t % 2
-        arrived, sem = x_out.at[t], x_sem.at[layer * 2 + q]
+        sent, sem = x_out.at[t], x_sem.at[layer * 2 + q]
         done(yb.at[t, q], y_sem.at[t * 2 + q])
-        slot = jnp.where(q == 1, 3, jnp.where(outer, 1, 2))
-        target = gb.at[layer, :, slot, x * 2 + c]
+        late = jnp.where(q == 1, 3, jnp.where(outer, 1, 2))
+        slot = jnp.where(t < LATE, late, jnp.where(outer, 1 - q, q))
+        target = gb.at[layer, slot, x * 2 + c]
         for step in (2, 1, 3):
             far = (x + step) % 4
-            send(yb.at[t, q, far], target, arrived, sem, at(far, y, z, core))
+            send(yb.at[t, q, far], target, sent, sem, at(far, y, z, core))
 
         @pl.when(core != c)
         def _():
-            send(yb.at[t, q, x], target, arrived, sem, at(x, y, z, 1 - c))
+            send(yb.at[t, q, x], target, sent, sem, at(x, y, z, 1 - c))
 
         @pl.when(core == c)
         def _():
             pltpu.make_async_copy(yb.at[t, q, x], target, sem).start()
 
-    def along_z(t, q):
-        layer = t // 2
-
+    def mine(t, stage):
         @pl.when(t % 2 == c)
         def _():
-            done(gb.at[layer, :, 2 + q], x_sem.at[layer * 2 + q])
-
-            @pl.when(inner | (q == 1))
-            def _():
-                slot = jnp.where(outer, 1, 0)
-                to = jnp.where(q == 1, 1 + z % 2, 3 * (z // 2))
-                target = gb.at[layer, :, slot]
-                send(gb.at[layer, :, 2 + q], target, z_out.at[layer], z_sem.at[layer * 2 + slot], at(x, y, to, c))
-
-    def finish(t, q):
-        layer = t // 2
-
-        @pl.when((t % 2 == c) & ((outer & (q == 0)) | (inner & (q == 1))))
-        def _():
-            done(gb.at[layer, :, 0], z_sem.at[layer * 2])
+            stage(t // 2)
+
+    def z_last(layer, q):
+        done(gb.at[layer, 2 + q], x_sem.at[layer * 2 + q])
+
+        @pl.when(q == 1)
+        def _():
+            target = gb.at[layer, jnp.where(outer, 2, 0)]
+            send(gb.at[layer, 3], target, z_out.at[layer], z_sem.at[layer * 2], far_z)
+
+        @pl.when((q == 0) & inner)
+        def _():
+            send(gb.at[layer, 2], gb.at[layer, 0], z_out.at[layer], z_sem.at[layer * 2 + 1], near_z)
+
+    def z_last_relay(layer):
+        @pl.when(outer)
+        def _():
+            done(gb.at[layer, 2], z_sem.at[layer * 2])
+            send(gb.at[layer, 2], gb.at[layer, 1], z_out.at[layer], z_sem.at[layer * 2 + 1], near_z)
+
+    def finish(layer, late):
+        if late:
+            done(gb.at[layer, 0], z_sem.at[layer * 2 + 1])
 
             @pl.when(inner)
             def _():
-                done(gb.at[layer, :, 1], z_sem.at[layer * 2 + 1])
-
-            gain = gv[pl.ds(layer, 1), :]
-            for pair in range(PAIRS):
-                arrived = gb[layer, pair, 0:2].reshape(256, FEATS)
-                rows = jnp.dot(rm[pair // 2], arrived, preferred_element_type=jnp.float32) * gain
-                ob[layer, pair * 256 : (pair + 1) * 256, :] = rows.astype(jnp.bfloat16)
-            pltpu.make_async_copy(ob.at[layer], out_ref.at[layer], o_sem.at[layer]).start()
+                done(gb.at[layer, 1], z_sem.at[layer * 2])
+
+        else:
+            done(gb.at[layer, 0], x_sem.at[layer * 2])
+            done(gb.at[layer, 1], x_sem.at[layer * 2 + 1])
+        gain = gv[pl.ds(layer, 1), :]
+        for pair in range(PAIRS):
+            arrived = gb[layer, 0:2, :, pair].reshape(256, FEATS)
+            rows = jnp.dot(rm[pair // 2], arrived, preferred_element_type=jnp.float32) * gain
+            ob[layer, pair * 256 : (pair + 1) * 256, :] = rows.astype(jnp.bfloat16)
+        pltpu.make_async_copy(ob.at[layer], out_ref.at[layer], o_sem.at[layer]).start()
+
+    sort_matrix(pm)
+    for n in range(AHEAD):
+        sort(n)
+    load_gain.wait()
+    load_rot.wait()
+    pl.semaphore_wait(barrier, 23)
+    for j in range(AHEAD // 2):
+        z_first(LATE + j)
+        along_y(j, 0)
+        along_y(j, 1)
 
     def share_gain():
         @pl.when(ma // 2 == dev)
@@ -195,7 +224,7 @@
         for half in range(2):
             size = None
             for core in range(2):
-                rows = sb[layer * 2 + core, place(half)].reshape(192, FEATS).astype(jnp.float32)
+                rows = sb[layer * 2 + core, place(layer * 2, half)].reshape(192, FEATS).astype(jnp.float32)
                 rows = jnp.abs(rows * gs[core, pl.ds(layer, 1), :])
                 rows = jnp.maximum(rows[:, :128], rows[:, 128:])
                 size = rows if size is None else jnp.maximum(size, rows)
@@ -245,33 +274,34 @@
                 line, rm[pair // 2], (((1,), (1,)), ((), ())), preferred_element_type=jnp.float32
             )
 
-    def order(u):
-        later = u - SKEW
-        even = later % 2 == 0
-        t = jnp.where(u < SKEW, u, jnp.where(u >= STEPS - SKEW, u - CHUNKS, jnp.where(even, later // 2, SKEW + later // 2)))
-        q = jnp.where(u < SKEW, 0, jnp.where(u >= STEPS - SKEW, 1, jnp.where(even, 1, 0)))
-        return t, q
-
     def turn(i, carry):
-        def during(lag, stage):
-            @pl.when((i >= lag) & (i < STEPS + lag))
+        def halves(at_step, stage, first, last):
+            v = i - at_step
+
+            @pl.when((v >= first) & (v < last))
             def _():
-                stage(*order(i - lag))
-
-        def keep_sorted(t, q):
-            @pl.when((q == 0) & (t + AHEAD < CHUNKS))
+                stage(v // 2, v % 2)
+
+        def chunks(at_step, stage, first, last):
+            v = i - at_step
+
+            @pl.when((v >= 2 * first) & (v < 2 * last) & (v % 2 == 0))
             def _():
-                sort(t + AHEAD)
-
-            @pl.when((q == 0) & (t > 0) & (t + AHEAD - 1 < CHUNKS))
-            def _():
-                swap(t + AHEAD - 1)
-
-        during(0, along_y)
-        during(LAG_X, along_x)
-        during(LAG_Z, along_z)
-        during(0, keep_sorted)
-        during(LAG_F, finish)
+                stage(v // 2)
+
+        halves(0, along_x, 0, STEPS)
+        halves(1 - AHEAD, along_y, AHEAD, STEPS)
+        chunks(2 - AHEAD, lambda j: z_first(LATE + j), AHEAD // 2, CHUNKS - LATE)
+        chunks(Z_FIRST_RELAY, lambda j: z_first_relay(LATE + j), 0, CHUNKS - LATE)
+        halves(Z_LAST, lambda t, q: mine(t, lambda layer: z_last(layer, q)), 0, 2 * LATE)
+        chunks(Z_LAST_RELAY, lambda t: mine(t, z_last_relay), 0, LATE)
+
+        @pl.when(i < CHUNKS - AHEAD)
+        def _():
+            sort(i + AHEAD)
+
+        chunks(FINISH_LATE, lambda t: mine(t, lambda layer: finish(layer, True)), 0, LATE)
+        chunks(FINISH, lambda j: mine(LATE + j, lambda layer: finish(layer, False)), 0, CHUNKS - LATE)
 
         @pl.when((i >= PEAKS_FROM) & (i < PEAKS_FROM + 2 * LAYERS) & (i % 2 == 0))
         def _():
@@ -289,14 +319,14 @@
 
         return carry
 
-    lax.fori_loop(0, STEPS + LAG_F, turn, 0)
+    lax.fori_loop(0, END, turn, 0)
 
     def close(t, carry):
         done(sb.at[t, 0:2, 0:3], y_out.at[t])
 
-        @pl.when(outer)
-        def _():
-            done(sb.at[t, 2], swap_out.at[t])
+        @pl.when(t >= LATE)
+        def _():
+            done(sb.at[t, 2:4], first_out.at[t])
 
         @pl.when(t % 2 == c)
         def _():
@@ -311,13 +341,9 @@
     lax.fori_loop(0, CHUNKS, close, 0)
 
     def close_layer(layer, carry):
-        @pl.when(outer)
-        def _():
-            done(gb.at[layer, :, 3], z_out.at[layer])
-
-        @pl.when(inner)
-        def _():
-            done(gb.at[layer, :, 2:4], z_out.at[layer])
+        @pl.when(layer < LATE // 2)
+        def _():
+            done(gb.at[layer, 2:4], z_out.at[layer])
 
         done(ob.at[layer], o_sem.at[layer])
         return carry
@@ -361,9 +387,9 @@
             pltpu.VMEM((LAYERS, FEATS), f32),
             pltpu.VMEM((15, LAYERS, FEATS), f32),
             pltpu.VMEM((CHUNKS, FEATS, COLS), bf16),
-            pltpu.VMEM((CHUNKS, 3, 4, PAIRS, 16, FEATS), bf16),
+            pltpu.VMEM((CHUNKS, 4, 4, PAIRS, 16, FEATS), bf16),
             pltpu.VMEM((CHUNKS, 2, 4, PAIRS, 16, FEATS), bf16),
-            pltpu.VMEM((LAYERS, PAIRS, 4, 8, 16, FEATS), bf16),
+            pltpu.VMEM((LAYERS, 4, 8, PAIRS, 16, FEATS), bf16),
             pltpu.VMEM((LAYERS, 768, FEATS), bf16),
             pltpu.VMEM((COLS, 128), f32),
             pltpu.VMEM((8, LAYERS, COLS), f32),
@@ -375,6 +401,7 @@
             dma,
             dma((2,)),
             dma,
+            dma((CHUNKS,)),
             dma((CHUNKS,)),
             dma((CHUNKS * 2,)),
             dma((LAYERS * 2,)),

time: 67.9 us -> 60 us (0.88)
  Pallas kernels: 66.7 us -> 59.2 us
    pallas_call x1, Pallas kernels: 65 us -> 57.5 us  [shards(): pl.pallas_call(kernel, name='relayout', out_shape=(jax.ShapeDtypeStruct((...]
where the time goes in v3:
time: 60 us; the launch traced here: 59.9 us
  Pallas kernels  59.2 us (99%)
  between operations  0.64 us (1%)
    pallas_call x1, Pallas kernels, shards(): pl.pallas_call(kernel, name='relayout', out_shape=(jax.ShapeDtypeStruct((...  57.5 us
    pallas_call x1, Pallas kernels, shards(): pl.pallas_call(write_out, name='write_out', out_shape=(jax.ShapeDtypeStru...  1.69 us

profile of v3, /device:TPU:1, one launch (start us, length us, event | category | flops | bytes accessed | tf_op | source)
XLA Modules:
  0.0 59.9 jit_solution(10389060657621907964)
XLA Ops:
  0.6 57.5 %relayout.1 = (bf16[8,768,256]{2,1,0:T(8,128)(2,1)S(1)}, f32[8,768]{1,0:T(8,128)S(1)}) custom-call(s32[1,128]{1,0:T(1,128)} %bitcast.1, f32[8,256]{1,0:T(8,128)} %gain_ref.1, bf16[8,512,384]{2,1,0:T(8,128)(2,1)} %w_ref.1), custom_call_target="tpu_custom_call" | custom-call | tf_op jit(solution)/shard_map/relayout/pallas_call | solution.py:379
  58.2 1.7 %write_out.1 = (bf16[8,512,256]{2,1,0:T(8,128)(2,1)}, bf16[8,128,256]{2,1,0:T(8,128)(2,1)}, bf16[8,128,256]{2,1,0:T(8,128)(2,1)}, f32[8,768]{1,0:T(8,128)}) custom-call(bf16[8,768,256]{2,1,0:T(8,128)(2,1)S(1)} %get-tuple-element.6.tiles_ref, f32[8,768]{1,0:T(8,128)S(1)} %get-tuple-element.7.peak_ref), custom_call_target="tpu_custom_call" | custom-call | tf_op jit(solution)/shard_map/write_out/pallas_call | solution.py:421

commit v4 on v3

--- a/solution.py
+++ b/solution.py
@@ -13,9 +13,11 @@
 PAIRS = 3
 LATE = 8
 AHEAD = 8
+LEAD = 7
+SHARE, MATRIX = 0, 2
 STEPS = 2 * CHUNKS
-Z_LAST, Z_LAST_RELAY, Z_FIRST_RELAY, FINISH_LATE, FINISH = 5, 20, 3, 25, 23
-PEAKS_FROM, PEAKS_SEND, PEAKS_GROUP, PEAKS_SPREAD, PEAKS_LAST = 10, 25, 29, 30, 34
+Z_LAST, Z_LAST_RELAY, Z_FIRST_RELAY, FINISH_LATE, FINISH = 7, 18, 3, 23, 21
+PEAKS_FROM, PEAKS_SEND, PEAKS_GROUP, PEAKS_SPREAD, PEAKS_LAST = 6, 14, 24, 25, 34
 END = max(FINISH, FINISH_LATE) + 15
 MESH = pl.DeviceIdType.MESH
 
@@ -195,16 +197,27 @@
             ob[layer, pair * 256 : (pair + 1) * 256, :] = rows.astype(jnp.bfloat16)
         pltpu.make_async_copy(ob.at[layer], out_ref.at[layer], o_sem.at[layer]).start()
 
+    def first_send(n):
+        @pl.when(n % 2 == 0)
+        def _():
+            along_y(n // 2, 0)
+            along_y(n // 2, 1)
+
+        @pl.when(n % 2 == 1)
+        def _():
+            z_first(LATE + n // 2)
+
+    def start(n, carry):
+        sort(n)
+        first_send(n - 1)
+        return carry
+
     sort_matrix(pm)
-    for n in range(AHEAD):
-        sort(n)
+    sort(0)
     load_gain.wait()
     load_rot.wait()
     pl.semaphore_wait(barrier, 23)
-    for j in range(AHEAD // 2):
-        z_first(LATE + j)
-        along_y(j, 0)
-        along_y(j, 1)
+    lax.fori_loop(1, AHEAD, start, 0)
 
     def share_gain():
         @pl.when(ma // 2 == dev)
@@ -290,8 +303,8 @@
                 stage(v // 2)
 
         halves(0, along_x, 0, STEPS)
-        halves(1 - AHEAD, along_y, AHEAD, STEPS)
-        chunks(2 - AHEAD, lambda j: z_first(LATE + j), AHEAD // 2, CHUNKS - LATE)
+        pl.when(i <= CHUNKS - AHEAD)(lambda: first_send(i + AHEAD - 1))
+        halves(-LEAD, along_y, 2 * LATE, STEPS)
         chunks(Z_FIRST_RELAY, lambda j: z_first_relay(LATE + j), 0, CHUNKS - LATE)
         halves(Z_LAST, lambda t, q: mine(t, lambda layer: z_last(layer, q)), 0, 2 * LATE)
         chunks(Z_LAST_RELAY, lambda t: mine(t, z_last_relay), 0, LATE)
@@ -303,19 +316,17 @@
         chunks(FINISH_LATE, lambda t: mine(t, lambda layer: finish(layer, True)), 0, LATE)
         chunks(FINISH, lambda j: mine(LATE + j, lambda layer: finish(layer, False)), 0, CHUNKS - LATE)
 
-        @pl.when((i >= PEAKS_FROM) & (i < PEAKS_FROM + 2 * LAYERS) & (i % 2 == 0))
-        def _():
-            peaks((i - PEAKS_FROM) // 2)
+        @pl.when((i >= PEAKS_FROM) & (i < PEAKS_FROM + LAYERS))
+        def _():
+            peaks(i - PEAKS_FROM)
 
         pl.when(i == PEAKS_SEND)(send_peaks)
         pl.when(i == PEAKS_GROUP)(group_peaks)
         pl.when(i == PEAKS_SPREAD)(spread_peaks)
         pl.when(i == PEAKS_LAST)(last_peaks)
 
-        @pl.when(i == 0)
-        def _():
-            share_gain()
-            order_matrix(rv, rm, zl)
+        pl.when(i == SHARE)(share_gain)
+        pl.when(i == MATRIX)(lambda: order_matrix(rv, rm, zl))
 
         return carry
 

time: 60 us -> 56.2 us (0.937)
  Pallas kernels: 59.2 us -> 55 us
    pallas_call x1, Pallas kernels: 57.5 us -> 53.4 us  [shards(): pl.pallas_call(kernel, name='relayout', out_shape=(jax.ShapeDtypeStruct((...]
where the time goes in v4:
time: 56.2 us; the launch traced here: 55.7 us
  Pallas kernels  55 us (98%)
  between operations  0.64 us (1%)
    pallas_call x1, Pallas kernels, shards(): pl.pallas_call(kernel, name='relayout', out_shape=(jax.ShapeDtypeStruct((...  53.4 us
    pallas_call x1, Pallas kernels, shards(): pl.pallas_call(write_out, name='write_out', out_shape=(jax.ShapeDtypeStru...  1.69 us

profile of v4, /device:TPU:1, one launch (start us, length us, event | category | flops | bytes accessed | tf_op | source)
XLA Modules:
  0.0 55.7 jit_solution(6830189122020688199)
XLA Ops:
  0.6 53.4 %relayout.1 = (bf16[8,768,256]{2,1,0:T(8,128)(2,1)S(1)}, f32[8,768]{1,0:T(8,128)S(1)}) custom-call(s32[1,128]{1,0:T(1,128)} %bitcast.1, f32[8,256]{1,0:T(8,128)} %gain_ref.1, bf16[8,512,384]{2,1,0:T(8,128)(2,1)} %w_ref.1), custom_call_target="tpu_custom_call" | custom-call | tf_op jit(solution)/shard_map/relayout/pallas_call | solution.py:390
  54.0 1.7 %write_out.1 = (bf16[8,512,256]{2,1,0:T(8,128)(2,1)}, bf16[8,128,256]{2,1,0:T(8,128)(2,1)}, bf16[8,128,256]{2,1,0:T(8,128)(2,1)}, f32[8,768]{1,0:T(8,128)}) custom-call(bf16[8,768,256]{2,1,0:T(8,128)(2,1)S(1)} %get-tuple-element.6.tiles_ref, f32[8,768]{1,0:T(8,128)S(1)} %get-tuple-element.7.peak_ref), custom_call_target="tpu_custom_call" | custom-call | tf_op jit(solution)/shard_map/write_out/pallas_call | solution.py:432

commit v5 on v4

--- a/solution.py
+++ b/solution.py
@@ -13,11 +13,11 @@
 PAIRS = 3
 LATE = 8
 AHEAD = 8
-LEAD = 7
-SHARE, MATRIX = 0, 2
+LEAD = 5
+SHARE, MATRIX, CLOSE = 0, 2, 5
 STEPS = 2 * CHUNKS
 Z_LAST, Z_LAST_RELAY, Z_FIRST_RELAY, FINISH_LATE, FINISH = 7, 18, 3, 23, 21
-PEAKS_FROM, PEAKS_SEND, PEAKS_GROUP, PEAKS_SPREAD, PEAKS_LAST = 6, 14, 24, 25, 34
+PEAKS_FROM, PEAKS_SEND, PEAKS_GROUP, PEAKS_SPREAD, PEAKS_LAST = 6, 15, 29, 30, 37
 END = max(FINISH, FINISH_LATE) + 15
 MESH = pl.DeviceIdType.MESH
 
@@ -57,8 +57,8 @@
 
 def kernel(
     rot_ref, gain_ref, w_ref, out_ref, peak_ref,
-    rv, gv, gs, xb, sb, yb, gb, ob, pt, pk1, pk2, pm, rm,
-    in_sem, rot_sem, gain_sem, gs_sem, gs_out, far_sem, near_sem, y_sem, x_sem, z_sem, first_out, y_out, x_out, z_out, o_sem,
+    rv, gv, gs, xb, sb, yb, gb, pt, pt2, pk0, pk1, pk2, pm, rm,
+    in_sem, rot_sem, gain_sem, gs_sem, gs_out, far_sem, near_sem, y_sem, x_sem, z_sem, first_out, y_out, x_out, z_out,
     pk1_sem, pk1_out, pk2_sem, pk2_out,
 ):
     dev, ma = lax.axis_index("dev"), lax.axis_index("ma")
@@ -194,8 +194,7 @@
         for pair in range(PAIRS):
             arrived = gb[layer, 0:2, :, pair].reshape(256, FEATS)
             rows = jnp.dot(rm[pair // 2], arrived, preferred_element_type=jnp.float32) * gain
-            ob[layer, pair * 256 : (pair + 1) * 256, :] = rows.astype(jnp.bfloat16)
-        pltpu.make_async_copy(ob.at[layer], out_ref.at[layer], o_sem.at[layer]).start()
+            out_ref[layer, pair * 256 : (pair + 1) * 256, :] = rows.astype(jnp.bfloat16)
 
     def first_send(n):
         @pl.when(n % 2 == 0)
@@ -249,19 +248,23 @@
         def _():
             for block in range(3):
                 lanes = slice(block * 128, (block + 1) * 128)
-                pk1[dev, :, lanes] = jnp.transpose(pt[lanes, :])[0:LAYERS, :].astype(jnp.bfloat16).astype(jnp.float32)
+                pt2[:, lanes] = jnp.transpose(pt[lanes, :])[0:LAYERS, :]
+
+    def split_peaks():
+        line = pt2[...]
+        for group in range(8):
+            part = pltpu.roll(line, COLS - group * PIECE, 1) if group else line
+            pk0[group] = part[:, 0:128].astype(jnp.bfloat16)
 
     def send_peaks():
+        pltpu.make_async_copy(pk0.at[dev], pk1.at[dev], pk1_sem).start()
         for step in range(1, 8):
-            send(pk1.at[dev], pk1.at[dev], pk1_out, pk1_sem, {"dev": (dev + step) % 8, "ma": ma})
+            to = (dev + step) % 8
+            send(pk0.at[to], pk1.at[dev], pk1_out, pk1_sem, {"dev": to, "ma": ma})
 
     def group_peaks():
-        done(pk1.at[0:7], pk1_sem)
-        top = jnp.max(pk1[...], axis=0).astype(jnp.bfloat16)
-        row = lax.broadcasted_iota(jnp.int32, (COLS, 128), 0)
-        lane = lax.broadcasted_iota(jnp.int32, (COLS, 128), 1)
-        pick = jnp.where((row - dev * PIECE == lane) & (lane < PIECE), 1.0, 0.0).astype(jnp.bfloat16)
-        pk2[ma] = jnp.dot(top, pick, preferred_element_type=jnp.float32)
+        done(pk1, pk1_sem)
+        pk2[ma] = jnp.max(pk1[...].astype(jnp.float32), axis=0).astype(jnp.bfloat16)
 
     def spread_peaks():
         for step in range(1, 16):
@@ -276,7 +279,7 @@
                 line = jnp.zeros((LAYERS, 128), jnp.float32)
                 for piece in range(8):
                     shift = (piece - pair) * 16 % 128
-                    part = pk2[half * 8 + piece]
+                    part = pk2[half * 8 + piece].astype(jnp.float32)
                     part = pltpu.roll(part, shift, 1) if shift else part
                     line = jnp.where((lane >= piece * 16) & (lane < piece * 16 + 16), part, line)
                 halves.append(line)
@@ -287,6 +290,21 @@
                 line, rm[pair // 2], (((1,), (1,)), ((), ())), preferred_element_type=jnp.float32
             )
 
+    def close(t):
+        done(sb.at[t, 0:2, 0:3], y_out.at[t])
+
+        @pl.when(t >= LATE)
+        def _():
+            done(sb.at[t, 2:4], first_out.at[t])
+
+        @pl.when(t % 2 == c)
+        def _():
+            done(yb.at[t, :, 0:3], x_out.at[t])
+
+        @pl.when(t % 2 != c)
+        def _():
+            done(yb.at[t], x_out.at[t])
+
     def turn(i, carry):
         def halves(at_step, stage, first, last):
             v = i - at_step
@@ -320,11 +338,13 @@
         def _():
             peaks(i - PEAKS_FROM)
 
+        pl.when(i == PEAKS_SEND - 1)(split_peaks)
         pl.when(i == PEAKS_SEND)(send_peaks)
         pl.when(i == PEAKS_GROUP)(group_peaks)
         pl.when(i == PEAKS_SPREAD)(spread_peaks)
         pl.when(i == PEAKS_LAST)(last_peaks)
 
+        chunks(CLOSE, close, 0, CHUNKS)
         pl.when(i == SHARE)(share_gain)
         pl.when(i == MATRIX)(lambda: order_matrix(rv, rm, zl))
 
@@ -332,31 +352,11 @@
 
     lax.fori_loop(0, END, turn, 0)
 
-    def close(t, carry):
-        done(sb.at[t, 0:2, 0:3], y_out.at[t])
-
-        @pl.when(t >= LATE)
-        def _():
-            done(sb.at[t, 2:4], first_out.at[t])
-
-        @pl.when(t % 2 == c)
-        def _():
-            done(yb.at[t, :, 0:3], x_out.at[t])
-
-        @pl.when(t % 2 != c)
-        def _():
-            done(yb.at[t], x_out.at[t])
-
-        return carry
-
-    lax.fori_loop(0, CHUNKS, close, 0)
-
     def close_layer(layer, carry):
         @pl.when(layer < LATE // 2)
         def _():
             done(gb.at[layer, 2:4], z_out.at[layer])
 
-        done(ob.at[layer], o_sem.at[layer])
         return carry
 
     lax.fori_loop(0, LAYERS, close_layer, 0)
@@ -392,7 +392,7 @@
         name="relayout",
         out_shape=(jax.ShapeDtypeStruct((LAYERS, 768, FEATS), bf16), jax.ShapeDtypeStruct((LAYERS, 768), f32)),
         in_specs=[hbm, hbm, hbm],
-        out_specs=(anywhere, pl.BlockSpec(memory_space=pltpu.VMEM)),
+        out_specs=(pl.BlockSpec(memory_space=pltpu.VMEM), pl.BlockSpec(memory_space=pltpu.VMEM)),
         scratch_shapes=[
             pltpu.VMEM((1, 128), jnp.int32),
             pltpu.VMEM((LAYERS, FEATS), f32),
@@ -401,10 +401,11 @@
             pltpu.VMEM((CHUNKS, 4, 4, PAIRS, 16, FEATS), bf16),
             pltpu.VMEM((CHUNKS, 2, 4, PAIRS, 16, FEATS), bf16),
             pltpu.VMEM((LAYERS, 4, 8, PAIRS, 16, FEATS), bf16),
-            pltpu.VMEM((LAYERS, 768, FEATS), bf16),
             pltpu.VMEM((COLS, 128), f32),
-            pltpu.VMEM((8, LAYERS, COLS), f32),
-            pltpu.VMEM((16, LAYERS, 128), f32),
+            pltpu.VMEM((LAYERS, COLS), f32),
+            pltpu.VMEM((8, LAYERS, 128), bf16),
+            pltpu.VMEM((8, LAYERS, 128), bf16),
+            pltpu.VMEM((16, LAYERS, 128), bf16),
             pltpu.VMEM((COLS, COLS), bf16),
             pltpu.VMEM((2, 256, 256), bf16),
             dma((CHUNKS,)),
@@ -420,7 +421,6 @@
             dma((CHUNKS,)),
             dma((CHUNKS,)),
             dma((CHUNKS,)),
-            dma((LAYERS,)),
             dma((LAYERS,)),
             dma,
             dma,

time: 56.2 us -> 55 us (0.979)
  Pallas kernels: 55 us -> 54.1 us
    pallas_call x1, Pallas kernels: 53.4 us -> 52.4 us  [shards(): pl.pallas_call(kernel, name='relayout', out_shape=(jax.ShapeDtypeStruct((...]
where the time goes in v5:
time: 55 us; the launch traced here: 54.7 us
  Pallas kernels  54.1 us (98%)
  between operations  0.64 us (1%)
    pallas_call x1, Pallas kernels, shards(): pl.pallas_call(kernel, name='relayout', out_shape=(jax.ShapeDtypeStruct((...  52.4 us
    pallas_call x1, Pallas kernels, shards(): pl.pallas_call(write_out, name='write_out', out_shape=(jax.ShapeDtypeStru...  1.69 us

profile of v5, /device:TPU:1, one launch (start us, length us, event | category | flops | bytes accessed | tf_op | source)
XLA Modules:
  0.0 54.7 jit_solution(9333390220308750648)
XLA Ops:
  0.6 52.4 %relayout.1 = (bf16[8,768,256]{2,1,0:T(8,128)(2,1)S(1)}, f32[8,768]{1,0:T(8,128)S(1)}) custom-call(s32[1,128]{1,0:T(1,128)} %bitcast.1, f32[8,256]{1,0:T(8,128)} %gain_ref.1, bf16[8,512,384]{2,1,0:T(8,128)(2,1)} %w_ref.1), custom_call_target="tpu_custom_call" | custom-call | tf_op jit(solution)/shard_map/relayout/pallas_call | solution.py:390
  53.0 1.7 %write_out.1 = (bf16[8,512,256]{2,1,0:T(8,128)(2,1)}, bf16[8,128,256]{2,1,0:T(8,128)(2,1)}, bf16[8,128,256]{2,1,0:T(8,128)(2,1)}, f32[8,768]{1,0:T(8,128)}) custom-call(bf16[8,768,256]{2,1,0:T(8,128)(2,1)S(1)} %get-tuple-element.6.tiles_ref, f32[8,768]{1,0:T(8,128)S(1)} %get-tuple-element.7.peak_ref), custom_call_target="tpu_custom_call" | custom-call | tf_op jit(solution)/shard_map/write_out/pallas_call | solution.py:432

commit v6 on v5

--- a/solution.py
+++ b/solution.py
@@ -80,7 +80,7 @@
         pltpu.make_async_copy(ref, ref, sem).wait()
 
     def load(t):
-        return pltpu.make_async_copy(w_ref.at[t // 2, pl.ds((t % 2) * FEATS, FEATS), :], xb.at[t], in_sem.at[t])
+        return pltpu.make_async_copy(w_ref.at[t // 2, pl.ds((1 - t % 2) * FEATS, FEATS), :], xb.at[t], in_sem.at[t])
 
     load_rot = pltpu.make_async_copy(rot_ref, rv, rot_sem)
     load_gain = pltpu.make_async_copy(gain_ref, gv, gain_sem)
@@ -138,7 +138,7 @@
             send(sb.at[t, q, far], yb.at[t, q, y], y_out.at[t], y_sem.at[t * 2 + q], at(x, far, z, c))
 
     def along_x(t, q):
-        layer, core = t // 2, t % 2
+        layer, core = t // 2, 1 - t % 2
         sent, sem = x_out.at[t], x_sem.at[layer * 2 + q]
         done(yb.at[t, q], y_sem.at[t * 2 + q])
         late = jnp.where(q == 1, 3, jnp.where(outer, 1, 2))
@@ -157,7 +157,7 @@
             pltpu.make_async_copy(yb.at[t, q, x], target, sem).start()
 
     def mine(t, stage):
-        @pl.when(t % 2 == c)
+        @pl.when(t % 2 != c)
         def _():
             stage(t // 2)
 
@@ -237,7 +237,7 @@
             size = None
             for core in range(2):
                 rows = sb[layer * 2 + core, place(layer * 2, half)].reshape(192, FEATS).astype(jnp.float32)
-                rows = jnp.abs(rows * gs[core, pl.ds(layer, 1), :])
+                rows = jnp.abs(rows * gs[1 - core, pl.ds(layer, 1), :])
                 rows = jnp.maximum(rows[:, :128], rows[:, 128:])
                 size = rows if size is None else jnp.maximum(size, rows)
             top = jnp.max(size, axis=1, keepdims=True)
@@ -297,11 +297,11 @@
         def _():
             done(sb.at[t, 2:4], first_out.at[t])
 
+        @pl.when(t % 2 != c)
+        def _():
+            done(yb.at[t, :, 0:3], x_out.at[t])
+
         @pl.when(t % 2 == c)
-        def _():
-            done(yb.at[t, :, 0:3], x_out.at[t])
-
-        @pl.when(t % 2 != c)
         def _():
             done(yb.at[t], x_out.at[t])
 

time: 55 us -> 54.1 us (0.984)
  Pallas kernels: 54.1 us -> 53.3 us
    pallas_call x1, Pallas kernels: 52.4 us -> 51.6 us  [shards(): pl.pallas_call(kernel, name='relayout', out_shape=(jax.ShapeDtypeStruct((...]
where the time goes in v6:
time: 54.1 us; the launch traced here: 54 us
  Pallas kernels  53.3 us (99%)
  between operations  0.64 us (1%)
    pallas_call x1, Pallas kernels, shards(): pl.pallas_call(kernel, name='relayout', out_shape=(jax.ShapeDtypeStruct((...  51.6 us
    pallas_call x1, Pallas kernels, shards(): pl.pallas_call(write_out, name='write_out', out_shape=(jax.ShapeDtypeStru...  1.69 us

profile of v6, /device:TPU:1, one launch (start us, length us, event | category | flops | bytes accessed | tf_op | source)
XLA Modules:
  0.0 54.0 jit_solution(11977501909805613540)
XLA Ops:
  0.6 51.6 %relayout.1 = (bf16[8,768,256]{2,1,0:T(8,128)(2,1)S(1)}, f32[8,768]{1,0:T(8,128)S(1)}) custom-call(s32[1,128]{1,0:T(1,128)} %bitcast.1, f32[8,256]{1,0:T(8,128)} %gain_ref.1, bf16[8,512,384]{2,1,0:T(8,128)(2,1)} %w_ref.1), custom_call_target="tpu_custom_call" | custom-call | tf_op jit(solution)/shard_map/relayout/pallas_call | solution.py:390
  52.3 1.7 %write_out.1 = (bf16[8,512,256]{2,1,0:T(8,128)(2,1)}, bf16[8,128,256]{2,1,0:T(8,128)(2,1)}, bf16[8,128,256]{2,1,0:T(8,128)(2,1)}, f32[8,768]{1,0:T(8,128)}) custom-call(bf16[8,768,256]{2,1,0:T(8,128)(2,1)S(1)} %get-tuple-element.6.tiles_ref, f32[8,768]{1,0:T(8,128)S(1)} %get-tuple-element.7.peak_ref), custom_call_target="tpu_custom_call" | custom-call | tf_op jit(solution)/shard_map/write_out/pallas_call | solution.py:432

commit v7 on v6

--- a/solution.py
+++ b/solution.py
@@ -17,7 +17,7 @@
 SHARE, MATRIX, CLOSE = 0, 2, 5
 STEPS = 2 * CHUNKS
 Z_LAST, Z_LAST_RELAY, Z_FIRST_RELAY, FINISH_LATE, FINISH = 7, 18, 3, 23, 21
-PEAKS_FROM, PEAKS_SEND, PEAKS_GROUP, PEAKS_SPREAD, PEAKS_LAST = 6, 15, 29, 30, 37
+PEAKS_FROM, PEAKS_SEND, PEAKS_GROUP, PEAKS_SPREAD, PEAKS_LAST = 6, 15, 28, 29, 36
 END = max(FINISH, FINISH_LATE) + 15
 MESH = pl.DeviceIdType.MESH
 
@@ -55,9 +55,17 @@
         rm_ref[1, 128:256, lanes] = hot(plain, 1, block)
 
 
+def serve(gb, rm, gv, layer, out_ref, place):
+    gain = gv[pl.ds(layer, 1), :]
+    for pair in range(PAIRS):
+        arrived = gb[layer, 0:2, :, pair].reshape(256, FEATS)
+        rows = jnp.dot(rm[pair // 2], arrived, preferred_element_type=jnp.float32) * gain
+        out_ref[place, pair * 256 : (pair + 1) * 256, :] = rows.astype(jnp.bfloat16)
+
+
 def kernel(
-    rot_ref, gain_ref, w_ref, out_ref, peak_ref,
-    rv, gv, gs, xb, sb, yb, gb, pt, pt2, pk0, pk1, pk2, pm, rm,
+    rot_ref, gain_ref, w_ref, out_ref, peak_ref, gb, rm, gv,
+    rv, gs, xb, sb, yb, pt, pt2, pk0, pk1, pk2, pm,
     in_sem, rot_sem, gain_sem, gs_sem, gs_out, far_sem, near_sem, y_sem, x_sem, z_sem, first_out, y_out, x_out, z_out,
     pk1_sem, pk1_out, pk2_sem, pk2_out,
 ):
@@ -190,11 +198,10 @@
         else:
             done(gb.at[layer, 0], x_sem.at[layer * 2])
             done(gb.at[layer, 1], x_sem.at[layer * 2 + 1])
-        gain = gv[pl.ds(layer, 1), :]
-        for pair in range(PAIRS):
-            arrived = gb[layer, 0:2, :, pair].reshape(256, FEATS)
-            rows = jnp.dot(rm[pair // 2], arrived, preferred_element_type=jnp.float32) * gain
-            out_ref[layer, pair * 256 : (pair + 1) * 256, :] = rows.astype(jnp.bfloat16)
+
+        @pl.when(layer != (LATE // 2 if late else LAYERS) - 1)
+        def _():
+            serve(gb, rm, gv, layer, out_ref, layer)
 
     def first_send(n):
         @pl.when(n % 2 == 0)
@@ -213,10 +220,10 @@
 
     sort_matrix(pm)
     sort(0)
+    pl.semaphore_wait(barrier, 23)
+    lax.fori_loop(1, AHEAD, start, 0)
     load_gain.wait()
     load_rot.wait()
-    pl.semaphore_wait(barrier, 23)
-    lax.fori_loop(1, AHEAD, start, 0)
 
     def share_gain():
         @pl.when(ma // 2 == dev)
@@ -369,45 +376,57 @@
     done(pk2.at[0:15], pk2_out)
 
 
-def write_out(tiles_ref, peak_ref, q_ref, k_ref, v_ref, row_ref, sem):
-    copies = [
-        pltpu.make_async_copy(tiles_ref.at[:, pl.ds(0, 512)], q_ref, sem.at[0]),
-        pltpu.make_async_copy(tiles_ref.at[:, pl.ds(512, 128)], k_ref, sem.at[1]),
-        pltpu.make_async_copy(tiles_ref.at[:, pl.ds(640, 128)], v_ref, sem.at[2]),
-        pltpu.make_async_copy(peak_ref, row_ref, sem.at[3]),
-    ]
-    for copy in copies:
-        copy.start()
-    for copy in copies:
-        copy.wait()
+def write_out(tiles_ref, peak_ref, gb, rm, gv, q_ref, k_ref, v_ref, row_ref, last, sem):
+    copies = []
+
+    def copy(src, dst):
+        copies.append(pltpu.make_async_copy(src, dst, sem.at[len(copies)]))
+        copies[-1].start()
+
+    def tiles(src, layers):
+        for out, first, count in ((q_ref, 0, 512), (k_ref, 512, 128), (v_ref, 640, 128)):
+            copy(src.at[:, pl.ds(first, count)], out.at[layers])
+
+    half = LATE // 2
+    for layers in (pl.ds(0, half - 1), pl.ds(half, LAYERS - half - 1)):
+        tiles(tiles_ref.at[layers], layers)
+    copy(peak_ref, row_ref)
+    for place, layer in enumerate((half - 1, LAYERS - 1)):
+        serve(gb, rm, gv, layer, last, place)
+        tiles(last.at[pl.ds(place, 1)], pl.ds(layer, 1))
+    for waited in copies:
+        waited.wait()
 
 
 def shards(joined_weight, norm_gain, rotary_order):
     dma = pltpu.SemaphoreType.DMA
     bf16, f32 = jnp.bfloat16, jnp.float32
     hbm = pl.BlockSpec(memory_space=pltpu.HBM)
-    anywhere = pl.BlockSpec(memory_space=pl.ANY)
-    tiles, peak = pl.pallas_call(
+    vmem = pl.BlockSpec(memory_space=pltpu.VMEM)
+    moved = pl.pallas_call(
         kernel,
         name="relayout",
-        out_shape=(jax.ShapeDtypeStruct((LAYERS, 768, FEATS), bf16), jax.ShapeDtypeStruct((LAYERS, 768), f32)),
+        out_shape=(
+            jax.ShapeDtypeStruct((LAYERS, 768, FEATS), bf16),
+            jax.ShapeDtypeStruct((LAYERS, 768), f32),
+            jax.ShapeDtypeStruct((LAYERS, 4, 8, PAIRS, 16, FEATS), bf16),
+            jax.ShapeDtypeStruct((2, 256, 256), bf16),
+            jax.ShapeDtypeStruct((LAYERS, FEATS), f32),
+        ),
         in_specs=[hbm, hbm, hbm],
-        out_specs=(pl.BlockSpec(memory_space=pltpu.VMEM), pl.BlockSpec(memory_space=pltpu.VMEM)),
+        out_specs=(vmem,) * 5,
         scratch_shapes=[
             pltpu.VMEM((1, 128), jnp.int32),
-            pltpu.VMEM((LAYERS, FEATS), f32),
             pltpu.VMEM((15, LAYERS, FEATS), f32),
             pltpu.VMEM((CHUNKS, FEATS, COLS), bf16),
             pltpu.VMEM((CHUNKS, 4, 4, PAIRS, 16, FEATS), bf16),
             pltpu.VMEM((CHUNKS, 2, 4, PAIRS, 16, FEATS), bf16),
-            pltpu.VMEM((LAYERS, 4, 8, PAIRS, 16, FEATS), bf16),
             pltpu.VMEM((COLS, 128), f32),
             pltpu.VMEM((LAYERS, COLS), f32),
             pltpu.VMEM((8, LAYERS, 128), bf16),
             pltpu.VMEM((8, LAYERS, 128), bf16),
             pltpu.VMEM((16, LAYERS, 128), bf16),
             pltpu.VMEM((COLS, COLS), bf16),
-            pltpu.VMEM((2, 256, 256), bf16),
             dma((CHUNKS,)),
             dma,
             dma,
@@ -438,11 +457,11 @@
             jax.ShapeDtypeStruct((LAYERS, 128, FEATS), bf16),
             jax.ShapeDtypeStruct((LAYERS, 768), f32),
         ),
-        in_specs=[anywhere, anywhere],
+        in_specs=[vmem] * 5,
         out_specs=(hbm, hbm, hbm, hbm),
-        scratch_shapes=[dma((4,))],
-        compiler_params=pltpu.CompilerParams(vmem_limit_bytes=2**20),
-    )(tiles, peak)
+        scratch_shapes=[pltpu.VMEM((2, 768, FEATS), bf16), dma((13,))],
+        compiler_params=pltpu.CompilerParams(vmem_limit_bytes=4 * 2**20),
+    )(*moved)
 
 
 def solution(mesh):

time: 54.1 us -> 53.7 us (level)
  no operation moved by 1% of the time
where the time goes in v7:
time: 53.7 us; the launch traced here: 53.6 us
  Pallas kernels  52.9 us (99%)
  between operations  0.64 us (1%)
    pallas_call x1, Pallas kernels, shards(): pl.pallas_call(kernel, name='relayout', out_shape=(jax.ShapeDtypeStruct((...  51.2 us
    pallas_call x1, Pallas kernels, shards(): pl.pallas_call(write_out, name='write_out', out_shape=(jax.ShapeDtypeStru...  1.78 us

profile of v7, /device:TPU:1, one launch (start us, length us, event | category | flops | bytes accessed | tf_op | source)
XLA Modules:
  0.0 53.6 jit_solution(14178998200870223300)
XLA Ops:
  0.6 51.2 %relayout.1 = (bf16[8,768,256]{2,1,0:T(8,128)(2,1)S(1)}, f32[8,768]{1,0:T(8,128)S(1)}, bf16[8,4,8,3,16,256]{5,4,3,2,1,0:T(8,128)(2,1)S(1)}, bf16[2,256,256]{2,1,0:T(8,128)(2,1)S(1)}, f32[8,256]{1,0:T(8,128)S(1)}) custom-call(s32[1,128]{1,0:T(1,128)} %bitcast.1, f32[8,256]{1,0:T(8,128)} %gain_ref.1, bf16[8,512,384]{2,1,0:T(8,128)(2,1)} %w_ref.1), custom_call_target="tpu_custom_call" | custom-call | tf_op jit(solution)/shard_map/relayout/pallas_call | solution.py:406
  51.8 1.8 %write_out.1 = (bf16[8,512,256]{2,1,0:T(8,128)(2,1)}, bf16[8,128,256]{2,1,0:T(8,128)(2,1)}, bf16[8,128,256]{2,1,0:T(8,128)(2,1)}, f32[8,768]{1,0:T(8,128)}) custom-call(bf16[8,768,256]{2,1,0:T(8,128)(2,1)S(1)} %get-tuple-element.9.tiles_ref, f32[8,768]{1,0:T(8,128)S(1)} %get-tuple-element.10.peak_ref, ...), custom_call_target="tpu_custom_call" | custom-call | tf_op jit(solution)/shard_map/write_out/pallas_call | solution.py:451

commit v8 on v7

--- a/solution.py
+++ b/solution.py
@@ -12,12 +12,12 @@
 PIECE = 48
 PAIRS = 3
 LATE = 8
-AHEAD = 8
+AHEAD = 10
 LEAD = 5
 SHARE, MATRIX, CLOSE = 0, 2, 5
 STEPS = 2 * CHUNKS
-Z_LAST, Z_LAST_RELAY, Z_FIRST_RELAY, FINISH_LATE, FINISH = 7, 18, 3, 23, 21
-PEAKS_FROM, PEAKS_SEND, PEAKS_GROUP, PEAKS_SPREAD, PEAKS_LAST = 6, 15, 28, 29, 36
+Z_LAST, Z_LAST_RELAY, Z_FIRST_RELAY, FINISH_LATE, FINISH = 7, 17, 3, 23, 21
+PEAKS_FROM, PEAKS_SEND, PEAKS_GROUP, PEAKS_SPREAD = 6, 15, 27, 28
 END = max(FINISH, FINISH_LATE) + 15
 MESH = pl.DeviceIdType.MESH
 
@@ -64,7 +64,7 @@
 
 
 def kernel(
-    rot_ref, gain_ref, w_ref, out_ref, peak_ref, gb, rm, gv,
+    rot_ref, gain_ref, w_ref, out_ref, pk3, gb, rm, gv,
     rv, gs, xb, sb, yb, pt, pt2, pk0, pk1, pk2, pm,
     in_sem, rot_sem, gain_sem, gs_sem, gs_out, far_sem, near_sem, y_sem, x_sem, z_sem, first_out, y_out, x_out, z_out,
     pk1_sem, pk1_out, pk2_sem, pk2_out,
@@ -271,31 +271,14 @@
 
     def group_peaks():
         done(pk1, pk1_sem)
-        pk2[ma] = jnp.max(pk1[...].astype(jnp.float32), axis=0).astype(jnp.bfloat16)
+        pk2[...] = jnp.max(pk1[...].astype(jnp.float32), axis=0).astype(jnp.bfloat16)
 
     def spread_peaks():
+        pltpu.make_async_copy(pk2, pk3.at[8 + ma % 8], pk2_sem).start()
         for step in range(1, 16):
-            send(pk2.at[ma], pk2.at[ma], pk2_out, pk2_sem, {"dev": dev, "ma": (ma + step) % 16})
-
-    def last_peaks():
-        done(pk2.at[0:15], pk2_sem)
-        lane = lax.broadcasted_iota(jnp.int32, (LAYERS, 128), 1)
-        for pair in range(PAIRS):
-            halves = []
-            for half in range(2):
-                line = jnp.zeros((LAYERS, 128), jnp.float32)
-                for piece in range(8):
-                    shift = (piece - pair) * 16 % 128
-                    part = pk2[half * 8 + piece].astype(jnp.float32)
-                    part = pltpu.roll(part, shift, 1) if shift else part
-                    line = jnp.where((lane >= piece * 16) & (lane < piece * 16 + 16), part, line)
-                halves.append(line)
-            low = jnp.where(zl == 1, halves[0], halves[1])
-            high = jnp.where(zl == 1, halves[1], halves[0])
-            line = jnp.concatenate([low, high], axis=1).astype(jnp.bfloat16)
-            peak_ref[:, pair * 256 : (pair + 1) * 256] = lax.dot_general(
-                line, rm[pair // 2], (((1,), (1,)), ((), ())), preferred_element_type=jnp.float32
-            )
+            to = (ma + step) % 16
+            place = jnp.where(to // 8 == zl, 8, 0) + ma % 8
+            send(pk2, pk3.at[place], pk2_out, pk2_sem, {"dev": dev, "ma": to})
 
     def close(t):
         done(sb.at[t, 0:2, 0:3], y_out.at[t])
@@ -349,7 +332,6 @@
         pl.when(i == PEAKS_SEND)(send_peaks)
         pl.when(i == PEAKS_GROUP)(group_peaks)
         pl.when(i == PEAKS_SPREAD)(spread_peaks)
-        pl.when(i == PEAKS_LAST)(last_peaks)
 
         chunks(CLOSE, close, 0, CHUNKS)
         pl.when(i == SHARE)(share_gain)
@@ -373,10 +355,29 @@
         done(gs.at[0:15], gs_out)
 
     done(pk1.at[0:7], pk1_out)
-    done(pk2.at[0:15], pk2_out)
-
-
-def write_out(tiles_ref, peak_ref, gb, rm, gv, q_ref, k_ref, v_ref, row_ref, last, sem):
+    done(pk3.at[0:15], pk2_out)
+    done(pk3, pk2_sem)
+
+
+def serve_peaks(pk3, rm, peak):
+    lane = lax.broadcasted_iota(jnp.int32, (LAYERS, 128), 1)
+    for pair in range(PAIRS):
+        lines = []
+        for half in range(2):
+            line = jnp.zeros((LAYERS, 128), jnp.float32)
+            for piece in range(8):
+                shift = (piece - pair) * 16 % 128
+                part = pk3[half * 8 + piece].astype(jnp.float32)
+                part = pltpu.roll(part, shift, 1) if shift else part
+                line = jnp.where((lane >= piece * 16) & (lane < piece * 16 + 16), part, line)
+            lines.append(line)
+        line = jnp.concatenate(lines, axis=1).astype(jnp.bfloat16)
+        peak[:, pair * 256 : (pair + 1) * 256] = lax.dot_general(
+            line, rm[pair // 2], (((1,), (1,)), ((), ())), preferred_element_type=jnp.float32
+        )
+
+
+def write_out(tiles_ref, pk3, gb, rm, gv, q_ref, k_ref, v_ref, row_ref, last, peak, sem):
     copies = []
 
     def copy(src, dst):
@@ -390,10 +391,11 @@
     half = LATE // 2
     for layers in (pl.ds(0, half - 1), pl.ds(half, LAYERS - half - 1)):
         tiles(tiles_ref.at[layers], layers)
-    copy(peak_ref, row_ref)
     for place, layer in enumerate((half - 1, LAYERS - 1)):
         serve(gb, rm, gv, layer, last, place)
         tiles(last.at[pl.ds(place, 1)], pl.ds(layer, 1))
+    serve_peaks(pk3, rm, peak)
+    copy(peak, row_ref)
     for waited in copies:
         waited.wait()
 
@@ -408,7 +410,7 @@
         name="relayout",
         out_shape=(
             jax.ShapeDtypeStruct((LAYERS, 768, FEATS), bf16),
-            jax.ShapeDtypeStruct((LAYERS, 768), f32),
+            jax.ShapeDtypeStruct((16, LAYERS, 128), bf16),
             jax.ShapeDtypeStruct((LAYERS, 4, 8, PAIRS, 16, FEATS), bf16),
             jax.ShapeDtypeStruct((2, 256, 256), bf16),
             jax.ShapeDtypeStruct((LAYERS, FEATS), f32),
@@ -425,7 +427,7 @@
             pltpu.VMEM((LAYERS, COLS), f32),
             pltpu.VMEM((8, LAYERS, 128), bf16),
             pltpu.VMEM((8, LAYERS, 128), bf16),
-            pltpu.VMEM((16, LAYERS, 128), bf16),
+            pltpu.VMEM((LAYERS, 128), bf16),
             pltpu.VMEM((COLS, COLS), bf16),
             dma((CHUNKS,)),
             dma,
@@ -459,7 +461,7 @@
         ),
         in_specs=[vmem] * 5,
         out_specs=(hbm, hbm, hbm, hbm),
-        scratch_shapes=[pltpu.VMEM((2, 768, FEATS), bf16), dma((13,))],
+        scratch_shapes=[pltpu.VMEM((2, 768, FEATS), bf16), pltpu.VMEM((LAYERS, 768), f32), dma((13,))],
         compiler_params=pltpu.CompilerParams(vmem_limit_bytes=4 * 2**20),
     )(*moved)
 

time: 53.7 us -> 53 us (0.987); the launches traced: 53.6 us -> 52.1 us
  Pallas kernels: 52.9 us -> 51.5 us
    pallas_call x1, Pallas kernels: 51.2 us -> 49.7 us  [shards(): pl.pallas_call(kernel, name='relayout', out_shape=(jax.ShapeDtypeStruct((...]
where the time goes in v8:
time: 53 us; the launch traced here: 52.1 us
  Pallas kernels  51.5 us (97%)
  between operations  0.64 us (1%)
    pallas_call x1, Pallas kernels, shards(): pl.pallas_call(kernel, name='relayout', out_shape=(jax.ShapeDtypeStruct((...  49.7 us
    pallas_call x1, Pallas kernels, shards(): pl.pallas_call(write_out, name='write_out', out_shape=(jax.ShapeDtypeStru...  1.77 us

profile of v8, /device:TPU:1, one launch (start us, length us, event | category | flops | bytes accessed | tf_op | source)
XLA Modules:
  0.0 52.1 jit_solution(5696028540514332964)
XLA Ops:
  0.6 49.7 %relayout.1 = (bf16[8,768,256]{2,1,0:T(8,128)(2,1)S(1)}, bf16[16,8,128]{2,1,0:T(8,128)(2,1)S(1)}, bf16[8,4,8,3,16,256]{5,4,3,2,1,0:T(8,128)(2,1)S(1)}, bf16[2,256,256]{2,1,0:T(8,128)(2,1)S(1)}, f32[8,256]{1,0:T(8,128)S(1)}) custom-call(s32[1,128]{1,0:T(1,128)} %bitcast.1, f32[8,256]{1,0:T(8,128)} %gain_ref.1, bf16[8,512,384]{2,1,0:T(8,128)(2,1)} %w_ref.1), custom_call_target="tpu_custom_call" | custom-call | tf_op jit(solution)/shard_map/relayout/pallas_call | solution.py:408
  50.3 1.8 %write_out.1 = (bf16[8,512,256]{2,1,0:T(8,128)(2,1)}, bf16[8,128,256]{2,1,0:T(8,128)(2,1)}, bf16[8,128,256]{2,1,0:T(8,128)(2,1)}, f32[8,768]{1,0:T(8,128)}) custom-call(bf16[8,768,256]{2,1,0:T(8,128)(2,1)S(1)} %get-tuple-element.9.tiles_ref, bf16[16,8,128]{2,1,0:T(8,128)(2,1)S(1)} %get-tuple-element.10.pk3, ...), custom_call_target="tpu_custom_call" | custom-call | tf_op jit(solution)/shard_map/write_out/pallas_call | solution.py:453

commit v9 on v8

--- a/solution.py
+++ b/solution.py
@@ -13,10 +13,10 @@
 PAIRS = 3
 LATE = 8
 AHEAD = 10
-LEAD = 5
+LEAD = 6
 SHARE, MATRIX, CLOSE = 0, 2, 5
 STEPS = 2 * CHUNKS
-Z_LAST, Z_LAST_RELAY, Z_FIRST_RELAY, FINISH_LATE, FINISH = 7, 17, 3, 23, 21
+Z_LAST, Z_LAST_RELAY, Z_FIRST_RELAY, FINISH_LATE, FINISH = 7, 17, 2, 22, 21
 PEAKS_FROM, PEAKS_SEND, PEAKS_GROUP, PEAKS_SPREAD = 6, 15, 27, 28
 END = max(FINISH, FINISH_LATE) + 15
 MESH = pl.DeviceIdType.MESH

time: 53 us -> 52.9 us (level); the launches traced: 52.1 us -> 52.6 us
  no operation moved by 1% of the time
where the time goes in v9:
time: 52.9 us; the launch traced here: 52.6 us
  Pallas kernels  52 us (98%)
  between operations  0.64 us (1%)
    pallas_call x1, Pallas kernels, shards(): pl.pallas_call(kernel, name='relayout', out_shape=(jax.ShapeDtypeStruct((...  50.2 us
    pallas_call x1, Pallas kernels, shards(): pl.pallas_call(write_out, name='write_out', out_shape=(jax.ShapeDtypeStru...  1.77 us

profile of v9, /device:TPU:1, one launch (start us, length us, event | category | flops | bytes accessed | tf_op | source)
XLA Modules:
  0.0 52.6 jit_solution(11497984660092871625)
XLA Ops:
  0.6 50.2 %relayout.1 = (bf16[8,768,256]{2,1,0:T(8,128)(2,1)S(1)}, bf16[16,8,128]{2,1,0:T(8,128)(2,1)S(1)}, bf16[8,4,8,3,16,256]{5,4,3,2,1,0:T(8,128)(2,1)S(1)}, bf16[2,256,256]{2,1,0:T(8,128)(2,1)S(1)}, f32[8,256]{1,0:T(8,128)S(1)}) custom-call(s32[1,128]{1,0:T(1,128)} %bitcast.1, f32[8,256]{1,0:T(8,128)} %gain_ref.1, bf16[8,512,384]{2,1,0:T(8,128)(2,1)} %w_ref.1), custom_call_target="tpu_custom_call" | custom-call | tf_op jit(solution)/shard_map/relayout/pallas_call | solution.py:408
  50.9 1.8 %write_out.1 = (bf16[8,512,256]{2,1,0:T(8,128)(2,1)}, bf16[8,128,256]{2,1,0:T(8,128)(2,1)}, bf16[8,128,256]{2,1,0:T(8,128)(2,1)}, f32[8,768]{1,0:T(8,128)}) custom-call(bf16[8,768,256]{2,1,0:T(8,128)(2,1)S(1)} %get-tuple-element.9.tiles_ref, bf16[16,8,128]{2,1,0:T(8,128)(2,1)S(1)} %get-tuple-element.10.pk3, ...), custom_call_target="tpu_custom_call" | custom-call | tf_op jit(solution)/shard_map/write_out/pallas_call | solution.py:453

commit v10 on v8

--- a/solution.py
+++ b/solution.py
@@ -16,7 +16,7 @@
 LEAD = 5
 SHARE, MATRIX, CLOSE = 0, 2, 5
 STEPS = 2 * CHUNKS
-Z_LAST, Z_LAST_RELAY, Z_FIRST_RELAY, FINISH_LATE, FINISH = 7, 17, 3, 23, 21
+Z_LAST, Z_LAST_RELAY, Z_FIRST_RELAY, FINISH_LATE, FINISH = 7, 16, 2, 22, 21
 PEAKS_FROM, PEAKS_SEND, PEAKS_GROUP, PEAKS_SPREAD = 6, 15, 27, 28
 END = max(FINISH, FINISH_LATE) + 15
 MESH = pl.DeviceIdType.MESH

time: 53 us -> 53 us (level)
  the two profiles are of different devices: /device:TPU:1 before, /device:TPU:0 now
where the time goes in v10:
time: 53 us; the launch traced here: 52.9 us
  Pallas kernels  52.2 us (98%)
  between operations  0.64 us (1%)
    pallas_call x1, Pallas kernels, shards(): pl.pallas_call(kernel, name='relayout', out_shape=(jax.ShapeDtypeStruct((...  50.5 us
    pallas_call x1, Pallas kernels, shards(): pl.pallas_call(write_out, name='write_out', out_shape=(jax.ShapeDtypeStru...  1.77 us

profile of v10, /device:TPU:0, one launch (start us, length us, event | category | flops | bytes accessed | tf_op | source)
XLA Modules:
  0.0 52.9 jit_solution(15579409294935707441)
XLA Ops:
  0.6 50.5 %relayout.1 = (bf16[8,768,256]{2,1,0:T(8,128)(2,1)S(1)}, bf16[16,8,128]{2,1,0:T(8,128)(2,1)S(1)}, bf16[8,4,8,3,16,256]{5,4,3,2,1,0:T(8,128)(2,1)S(1)}, bf16[2,256,256]{2,1,0:T(8,128)(2,1)S(1)}, f32[8,256]{1,0:T(8,128)S(1)}) custom-call(s32[1,128]{1,0:T(1,128)} %bitcast.1, f32[8,256]{1,0:T(8,128)} %gain_ref.1, bf16[8,512,384]{2,1,0:T(8,128)(2,1)} %w_ref.1), custom_call_target="tpu_custom_call" | custom-call | tf_op jit(solution)/shard_map/relayout/pallas_call | solution.py:408
  51.1 1.8 %write_out.1 = (bf16[8,512,256]{2,1,0:T(8,128)(2,1)}, bf16[8,128,256]{2,1,0:T(8,128)(2,1)}, bf16[8,128,256]{2,1,0:T(8,128)(2,1)}, f32[8,768]{1,0:T(8,128)}) custom-call(bf16[8,768,256]{2,1,0:T(8,128)(2,1)S(1)} %get-tuple-element.9.tiles_ref, bf16[16,8,128]{2,1,0:T(8,128)(2,1)S(1)} %get-tuple-element.10.pk3, ...), custom_call_target="tpu_custom_call" | custom-call | tf_op jit(solution)/shard_map/write_out/pallas_call | solution.py:453
